TPU v7x, 16 devices: a whole 2x2x2 slice. The times are simulated.
16 devices in a mesh: terms: 16 (over z, y, x, core).
Axes of the slice: x: 2, y: 2, z: 2, core: 2. Of those that a mesh axis runs over, the one named last changes fastest.
Arguments:
- wavefunction: float32 [384, 16, 384], replicated
- left_env: bfloat16 [64, 384, 384], P('terms')
- pair_ops: bfloat16 [64, 16, 16], P('terms')
- right_env: bfloat16 [64, 384, 384], P('terms')
- full_term: int32 [64], P('terms')
Outputs:
- output 1: float32 [7, 384, 16, 384], P(None, 'terms')
- output 2: float32 [6], replicated
- output 3: float32 [6], replicated
All inputs are finite; a program needn't handle non-finite values.
Results may differ from a plain program's by a relative error of at most 0.0127149.
Values are sent between devices in bfloat16 or wider.
A program may use at most 1 GiB of HBM per device.

v0:
```python
import jax
import jax.numpy as jnp
from jax import lax
from jax.sharding import PartitionSpec as P

LANCZOS_STEPS = 6
AXIS_NAME = 'terms'


def local_sigma(vec_bf, left_loc, pair_loc, right_loc, flag_loc):
    def apply_right(right_env):
        return lax.dot_general(vec_bf, right_env, (((2,), (1,)), ((), ())), preferred_element_type=jnp.float32).astype(jnp.bfloat16)

    def keep_vector(right_env):
        return vec_bf

    def term_body(term_idx, running_sum):
        right_done = lax.cond(flag_loc[term_idx] == 1, apply_right, keep_vector, right_loc[term_idx])
        pair_done = lax.dot_general(pair_loc[term_idx], right_done, (((1,), (1,)), ((), ())), preferred_element_type=jnp.float32).astype(jnp.bfloat16)
        return running_sum + lax.dot_general(left_loc[term_idx], pair_done, (((1,), (1,)), ((), ())), preferred_element_type=jnp.float32)

    start_sum = jnp.zeros(vec_bf.shape, jnp.float32)
    return lax.fori_loop(0, left_loc.shape[0], term_body, start_sum)


def solution(mesh):
    group_size = mesh.shape[AXIS_NAME]

    def device_body(wavefunction, left_loc, pair_loc, right_loc, flag_loc):
        bond_dim = wavefunction.shape[0]
        vec_size = wavefunction.size
        slab_rows = bond_dim // group_size
        row_start = lax.axis_index(AXIS_NAME) * slab_rows
        first_vec = wavefunction / jnp.sqrt(jnp.sum(wavefunction * wavefunction) / vec_size)
        whole_bf = first_vec.astype(jnp.bfloat16)
        current = lax.dynamic_slice_in_dim(first_vec, row_start, slab_rows, axis=0)
        previous = jnp.zeros_like(current)
        beta_prev = jnp.zeros((), jnp.float32)
        slab_list = [current]
        alpha_list = []
        beta_list = []
        for step_num in range(LANCZOS_STEPS):
            part_sigma = local_sigma(whole_bf, left_loc, pair_loc, right_loc, flag_loc)
            sigma_slab = lax.psum_scatter(part_sigma, AXIS_NAME, scatter_dimension=0, tiled=True)
            alpha_now = lax.psum(jnp.sum(sigma_slab * current), AXIS_NAME) / vec_size
            residual = sigma_slab - alpha_now * current - beta_prev * previous
            beta_now = jnp.sqrt(lax.psum(jnp.sum(residual * residual), AXIS_NAME) / vec_size)
            following = residual / beta_now
            slab_list.append(following)
            alpha_list.append(alpha_now)
            beta_list.append(beta_now)
            if step_num + 1 < LANCZOS_STEPS:
                whole_bf = lax.all_gather(following.astype(jnp.bfloat16), AXIS_NAME, axis=0, tiled=True)
            previous, current, beta_prev = current, following, beta_now
        return jnp.stack(slab_list), jnp.stack(alpha_list), jnp.stack(beta_list)

    return jax.shard_map(device_body, mesh=mesh, in_specs=(P(), P(AXIS_NAME), P(AXIS_NAME), P(AXIS_NAME), P(AXIS_NAME)), out_specs=(P(None, AXIS_NAME), P(), P()), check_vma=False)
```

profile of v0, /device:TPU:0, one launch (start us, length us, event | category | flops | bytes accessed | tf_op | source)
XLA Modules:
  0.0 1983.4 jit_solution(820969143640183308)
XLA Ops:
  26.2 95.9 %while.84 = (s32[]{:T(128)}, f32[384,16,384]{2,0,1:T(8,128)}, bf16[4,384,384]{2,1,0:T(8,128)(2,1)S(1)}, bf16[4,16,16]{2,1,0:T(8,128)(2,1)S(1)}, s32[4]{0:T(128)S...) while((s32[]{:T(128)}, f32[384,16,384]{2,0,1:T(8,128)}, ...), condition=%wide.region_4.0_spmd.clone, body=%wide.region_1.0_spmd.clone.sunk | while | flops 3708813312 | bytes 52498620 | solution.py:23
  63.6 9.8 select_add_fusion.12
  112.2 9.8 select_add_fusion.12
  122.1 12.9 copy.63
  135.1 108.6 %reduce-scatter.7.cloned.1.call-done = f32[24,16,384]{2,1,0:T(8,128)} async-done(((f32[384,16,384]{2,1,0:T(8,128)}), f32[24,16,384]{2,1,0:T(8,128)}) %reduce-scatter.7.cloned.1.call-update) | async-done | bytes 589840 | tf_op jit(solution)/shard_map/reduce_scatter | solution.py:44
  245.7 31.9 %psum.84 = f32[]{:T(128)} all-reduce(f32[]{:T(128)} %multiply_reduce_fusion.12), channel_id=1, replica_groups=mesh['terms'=16] {'terms'}, use_global_device_ids=true, to_apply=%region_7.0 | all-reduce | flops 1 | bytes 8 | tf_op jit(solution)/shard_map/psum | solution.py:45
  280.2 32.7 %psum.85 = f32[]{:T(128)} all-reduce(f32[]{:T(128)} %multiply_reduce_fusion.11), channel_id=1, replica_groups=mesh['terms'=16] {'terms'}, use_global_device_ids=true, to_apply=%region_9.0 | all-reduce | flops 1 | bytes 8 | tf_op jit(solution)/shard_map/psum | solution.py:47
  315.8 37.6 %all-gather.6.cloned.1.call-done = bf16[384,16,384]{2,1,0:T(8,128)(2,1)} async-done(((bf16[24,16,384]{2,1,0:T(8,128)(2,1)}), bf16[384,16,384]{2,1,0:T(8,128)(2,1)}) %all-gather.6.cloned.1.call-update) | async-done | bytes 4718608 | tf_op jit(solution)/shard_map/all_gather | solution.py:53
  359.0 96.1 %while.85 = (s32[]{:T(128)}, f32[384,16,384]{2,0,1:T(8,128)}, bf16[4,384,384]{2,1,0:T(8,128)(2,1)S(1)}, bf16[4,16,16]{2,1,0:T(8,128)(2,1)S(1)}, s32[4]{0:T(128)S...) while((s32[]{:T(128)}, f32[384,16,384]{2,0,1:T(8,128)}, ...), condition=%wide.region_13.0_spmd.clone, body=%wide.region_10.0_spmd.clone.sunk | while | flops 3708813312 | bytes 52498620 | solution.py:23
  396.5 9.8 select_add_fusion.13
  420.8 9.8 select_add_fusion.13
  455.1 12.9 copy.65
  468.1 107.1 %reduce-scatter.9.cloned.1.call-done = f32[24,16,384]{2,1,0:T(8,128)} async-done(((f32[384,16,384]{2,1,0:T(8,128)}), f32[24,16,384]{2,1,0:T(8,128)}) %reduce-scatter.9.cloned.1.call-update) | async-done | bytes 589840 | tf_op jit(solution)/shard_map/reduce_scatter | solution.py:44
  577.0 31.9 %psum.86 = f32[]{:T(128)} all-reduce(f32[]{:T(128)} %multiply_reduce_fusion.10), channel_id=1, replica_groups=mesh['terms'=16] {'terms'}, use_global_device_ids=true, to_apply=%region_16.0 | all-reduce | flops 1 | bytes 8 | tf_op jit(solution)/shard_map/psum | solution.py:45
  611.5 32.7 %psum.87 = f32[]{:T(128)} all-reduce(f32[]{:T(128)} %get-tuple-element.1283), channel_id=1, replica_groups=mesh['terms'=16] {'terms'}, use_global_device_ids=true, to_apply=%region_18.0 | all-reduce | flops 1 | bytes 8 | tf_op jit(solution)/shard_map/psum | solution.py:47
  645.8 37.6 %all-gather.8.cloned.1.call-done = bf16[384,16,384]{2,1,0:T(8,128)(2,1)} async-done(((bf16[24,16,384]{2,1,0:T(8,128)(2,1)}), bf16[384,16,384]{2,1,0:T(8,128)(2,1)}) %all-gather.8.cloned.1.call-update) | async-done | bytes 4718608 | tf_op jit(solution)/shard_map/all_gather | solution.py:53
  689.0 96.3 %while.86 = (s32[]{:T(128)}, f32[384,16,384]{2,0,1:T(8,128)}, bf16[4,384,384]{2,1,0:T(8,128)(2,1)S(1)}, bf16[4,16,16]{2,1,0:T(8,128)(2,1)S(1)}, s32[4]{0:T(128)S...) while((s32[]{:T(128)}, f32[384,16,384]{2,0,1:T(8,128)}, ...), condition=%wide.region_22.0_spmd.clone, body=%wide.region_19.0_spmd.clone.sunk | while | flops 3708813312 | bytes 52498620 | solution.py:23
  751.0 9.8 select_add_fusion.14
  775.3 9.8 select_add_fusion.14
  785.3 12.9 copy.67
  798.2 107.0 %reduce-scatter.11.cloned.1.call-done = f32[24,16,384]{2,1,0:T(8,128)} async-done(((f32[384,16,384]{2,1,0:T(8,128)}), f32[24,16,384]{2,1,0:T(8,128)}) %reduce-scatter.11.cloned.1.call-update) | async-done | bytes 589840 | tf_op jit(solution)/shard_map/reduce_scatter | solution.py:44
  907.1 31.9 %psum.88 = f32[]{:T(128)} all-reduce(f32[]{:T(128)} %multiply_reduce_fusion.8), channel_id=1, replica_groups=mesh['terms'=16] {'terms'}, use_global_device_ids=true, to_apply=%region_25.0 | all-reduce | flops 1 | bytes 8 | tf_op jit(solution)/shard_map/psum | solution.py:45
  941.7 32.7 %psum.89 = f32[]{:T(128)} all-reduce(f32[]{:T(128)} %get-tuple-element.1281), channel_id=1, replica_groups=mesh['terms'=16] {'terms'}, use_global_device_ids=true, to_apply=%region_27.0 | all-reduce | flops 1 | bytes 8 | tf_op jit(solution)/shard_map/psum | solution.py:47
  975.9 37.6 %all-gather.10.cloned.1.call-done = bf16[384,16,384]{2,1,0:T(8,128)(2,1)} async-done(((bf16[24,16,384]{2,1,0:T(8,128)(2,1)}), bf16[384,16,384]{2,1,0:T(8,128)(2,1)}) %all-gather.10.cloned.1.call-update) | async-done | bytes 4718608 | tf_op jit(solution)/shard_map/all_gather | solution.py:53
  1019.1 98.7 %while.87 = (s32[]{:T(128)}, f32[384,16,384]{2,0,1:T(8,128)}, bf16[4,384,384]{2,1,0:T(8,128)(2,1)S(1)}, bf16[4,16,16]{2,1,0:T(8,128)(2,1)S(1)}, s32[4]{0:T(128)}...) while((s32[]{:T(128)}, f32[384,16,384]{2,0,1:T(8,128)}, ...), condition=%wide.region_31.0_spmd.clone, body=%wide.region_28.0_spmd.clone.sunk | while | flops 3708813312 | bytes 52498620 | solution.py:23
  1057.9 9.8 select_add_fusion.15
  1117.8 12.9 copy.69
  1130.7 107.0 %reduce-scatter.13.cloned.1.call-done = f32[24,16,384]{2,1,0:T(8,128)} async-done(((f32[384,16,384]{2,1,0:T(8,128)}), f32[24,16,384]{2,1,0:T(8,128)}) %reduce-scatter.13.cloned.1.call-update) | async-done | bytes 589840 | tf_op jit(solution)/shard_map/reduce_scatter | solution.py:44
  1239.6 31.9 %psum.90 = f32[]{:T(128)} all-reduce(f32[]{:T(128)} %multiply_reduce_fusion.6), channel_id=1, replica_groups=mesh['terms'=16] {'terms'}, use_global_device_ids=true, to_apply=%region_34.0 | all-reduce | flops 1 | bytes 8 | tf_op jit(solution)/shard_map/psum | solution.py:45
  1274.8 32.7 %psum.91 = f32[]{:T(128)} all-reduce(f32[]{:T(128)} %get-tuple-element.1279), channel_id=1, replica_groups=mesh['terms'=16] {'terms'}, use_global_device_ids=true, to_apply=%region_36.0 | all-reduce | flops 1 | bytes 8 | tf_op jit(solution)/shard_map/psum | solution.py:47
  1310.2 37.6 %all-gather.12.cloned.1.call-done = bf16[384,16,384]{2,1,0:T(8,128)(2,1)} async-done(((bf16[24,16,384]{2,1,0:T(8,128)(2,1)}), bf16[384,16,384]{2,1,0:T(8,128)(2,1)}) %all-gather.12.cloned.1.call-update) | async-done | bytes 4718608 | tf_op jit(solution)/shard_map/all_gather | solution.py:53
  1353.3 96.0 %while.88 = (s32[]{:T(128)}, f32[384,16,384]{2,0,1:T(8,128)}, bf16[4,384,384]{2,1,0:T(8,128)(2,1)S(1)}, bf16[4,16,16]{2,1,0:T(8,128)(2,1)S(1)}, s32[4]{0:T(128)S...) while((s32[]{:T(128)}, f32[384,16,384]{2,0,1:T(8,128)}, ...), condition=%wide.region_40.0_spmd.clone, body=%wide.region_37.0_spmd.clone.sunk | while | flops 3708813312 | bytes 52498620 | solution.py:23
  1390.9 9.8 select_add_fusion.16
  1415.1 9.8 select_add_fusion.16
  1439.3 9.8 select_add_fusion.16
  1449.3 12.9 copy.71
  1462.3 107.0 %reduce-scatter.15.cloned.1.call-done = f32[24,16,384]{2,1,0:T(8,128)} async-done(((f32[384,16,384]{2,1,0:T(8,128)}), f32[24,16,384]{2,1,0:T(8,128)}) %reduce-scatter.15.cloned.1.call-update) | async-done | bytes 589840 | tf_op jit(solution)/shard_map/reduce_scatter | solution.py:44
  1571.1 31.9 %psum.92 = f32[]{:T(128)} all-reduce(f32[]{:T(128)} %multiply_reduce_fusion.4), channel_id=1, replica_groups=mesh['terms'=16] {'terms'}, use_global_device_ids=true, to_apply=%region_43.0 | all-reduce | flops 1 | bytes 8 | tf_op jit(solution)/shard_map/psum | solution.py:45
  1606.4 32.7 %psum.93 = f32[]{:T(128)} all-reduce(f32[]{:T(128)} %get-tuple-element.1277), channel_id=1, replica_groups=mesh['terms'=16] {'terms'}, use_global_device_ids=true, to_apply=%region_45.0 | all-reduce | flops 1 | bytes 8 | tf_op jit(solution)/shard_map/psum | solution.py:47
  1641.7 37.6 %all-gather.14.cloned.1.call-done = bf16[384,16,384]{2,1,0:T(8,128)(2,1)} async-done(((bf16[24,16,384]{2,1,0:T(8,128)(2,1)}), bf16[384,16,384]{2,1,0:T(8,128)(2,1)}) %all-gather.14.cloned.1.call-update) | async-done | bytes 4718608 | tf_op jit(solution)/shard_map/all_gather | solution.py:53
  1685.0 99.0 %while.89 = (s32[]{:T(128)}, f32[384,16,384]{2,0,1:T(8,128)}, bf16[4,384,384]{2,1,0:T(8,128)(2,1)S(1)}, bf16[4,16,16]{2,1,0:T(8,128)(2,1)S(1)}, s32[4]{0:T(128)}...) while((s32[]{:T(128)}, f32[384,16,384]{2,0,1:T(8,128)}, ...), condition=%wide.region_49.0_spmd.clone, body=%wide.region_46.0_spmd.clone.sunk | while | flops 3708813312 | bytes 52498620 | solution.py:23
  1723.7 10.0 select_add_fusion.17
  1748.7 10.0 select_add_fusion.17
  1773.7 10.0 select_add_fusion.17
  1783.9 12.9 copy.73
  1802.3 101.6 %reduce-scatter.17.cloned.1.call-done = f32[24,16,384]{2,1,0:T(8,128)} async-done(((f32[384,16,384]{2,1,0:T(8,128)}), f32[24,16,384]{2,1,0:T(8,128)}) %reduce-scatter.17.cloned.1.call-update) | async-done | bytes 589840 | tf_op jit(solution)/shard_map/reduce_scatter | solution.py:44
  1906.6 31.9 %psum.94 = f32[]{:T(128)} all-reduce(f32[]{:T(128)} %multiply_reduce_fusion.2), channel_id=1, replica_groups=mesh['terms'=16] {'terms'}, use_global_device_ids=true, to_apply=%region_52.0 | all-reduce | flops 1 | bytes 8 | tf_op jit(solution)/shard_map/psum | solution.py:45
  1941.0 32.7 %psum.95 = f32[]{:T(128)} all-reduce(f32[]{:T(128)} %get-tuple-element.1275), channel_id=1, replica_groups=mesh['terms'=16] {'terms'}, use_global_device_ids=true, to_apply=%region_54.0 | all-reduce | flops 1 | bytes 8 | tf_op jit(solution)/shard_map/psum | solution.py:47
  (195 shorter events, 697.5 us)
Async XLA Ops:
  7.2 236.5 %reduce-scatter.7.cloned.1.call-start = ((), (), s32[]{:S(2)}) async-start(), calls=%async_computation.6 | async-start | bytes 10027008 | tf_op jit(solution)/shard_map/reduce_scatter | solution.py:44
  23.0 3.3 copy-start
  23.0 3.3 copy-start.1
  23.0 3.3 copy-start.8
  23.0 3.3 copy-start.9
  135.0 218.3 %all-gather.6.cloned.1.call-start = ((), (), s32[]{:S(2)}) async-start(), calls=%async_computation.7 | async-start | bytes 5013504 | tf_op jit(solution)/shard_map/all_gather | solution.py:53
  315.7 293.8 %copy-start.5 = (f32[24,16,384]{2,1,0:T(8,128)}, f32[24,16,384]{2,1,0:T(8,128)S(1)}, u32[]{:S(2)}) copy-start(f32[24,16,384]{2,1,0:T(8,128)S(1)} %get-tuple-element.1286) | copy-start | bytes 1769476
  315.7 259.5 %reduce-scatter.9.cloned.1.call-start = ((), (), s32[]{:S(2)}) async-start(), calls=%async_computation.8 | async-start | bytes 10027008 | tf_op jit(solution)/shard_map/reduce_scatter | solution.py:44
  455.1 12.9 copy-start.10
  468.0 215.3 %all-gather.8.cloned.1.call-start = ((), (), s32[]{:S(2)}) async-start(), calls=%async_computation.9 | async-start | bytes 5013504 | tf_op jit(solution)/shard_map/all_gather | solution.py:53
  611.5 660.6 %copy-start.2 = (f32[24,16,384]{2,1,0:T(8,128)}, f32[24,16,384]{2,1,0:T(8,128)S(1)}, u32[]{:S(2)}) copy-start(f32[24,16,384]{2,1,0:T(8,128)S(1)} %get-tuple-element.1284) | copy-start | bytes 1769476
  645.7 259.6 %reduce-scatter.11.cloned.1.call-start = ((), (), s32[]{:S(2)}) async-start(), calls=%async_computation.10 | async-start | bytes 10027008 | tf_op jit(solution)/shard_map/reduce_scatter | solution.py:44
  645.8 43.2 %copy-start.11 = (s32[4]{0:T(128)S(1)}, s32[4]{0:T(128)}, u32[]{:S(2)}) copy-start(s32[4]{0:T(128)} %copy-done.10) | copy-start | bytes 52
  798.2 215.3 %all-gather.10.cloned.1.call-start = ((), (), s32[]{:S(2)}) async-start(), calls=%async_computation.11 | async-start | bytes 5013504 | tf_op jit(solution)/shard_map/all_gather | solution.py:53
  975.9 261.9 %reduce-scatter.13.cloned.1.call-start = ((), (), s32[]{:S(2)}) async-start(), calls=%async_computation.12 | async-start | bytes 10027008 | tf_op jit(solution)/shard_map/reduce_scatter | solution.py:44
  1130.7 217.0 %all-gather.12.cloned.1.call-start = ((), (), s32[]{:S(2)}) async-start(), calls=%async_computation.13 | async-start | bytes 5013504 | tf_op jit(solution)/shard_map/all_gather | solution.py:53
  1310.1 259.2 %reduce-scatter.15.cloned.1.call-start = ((), (), s32[]{:S(2)}) async-start(), calls=%async_computation.14 | async-start | bytes 10027008 | tf_op jit(solution)/shard_map/reduce_scatter | solution.py:44
  1310.1 43.2 %copy-start.12 = (s32[4]{0:T(128)S(1)}, s32[4]{0:T(128)}, u32[]{:S(2)}) copy-start(s32[4]{0:T(128)} %get-tuple-element.1813) | copy-start | bytes 52
  1462.2 107.1 %copy-start.4 = (f32[24,16,384]{2,1,0:T(8,128)S(1)}, f32[24,16,384]{2,1,0:T(8,128)}, u32[]{:S(2)}) copy-start(f32[24,16,384]{2,1,0:T(8,128)} %get-tuple-element.1280) | copy-start | bytes 1769476
  1462.2 217.0 %all-gather.14.cloned.1.call-start = ((), (), s32[]{:S(2)}) async-start(), calls=%async_computation.15 | async-start | bytes 5013504 | tf_op jit(solution)/shard_map/all_gather | solution.py:53
  1641.6 262.3 %reduce-scatter.17.cloned.1.call-start = ((), (), s32[]{:S(2)}) async-start(), calls=%async_computation.16 | async-start | bytes 10027008 | tf_op jit(solution)/shard_map/reduce_scatter | solution.py:44
  1796.8 2.1 copy-start.6
  1796.8 2.9 copy-start.3
  1796.8 107.1 %copy-start.7 = (f32[24,16,384]{2,1,0:T(8,128)S(1)}, f32[24,16,384]{2,1,0:T(8,128)}, u32[]{:S(2)}) copy-start(f32[24,16,384]{2,1,0:T(8,128)} %get-tuple-element.1278) | copy-start | bytes 1769476
Sparse Core Ops, SparseCore 0:
  135.1 108.4 reduce-scatter.6
  315.8 37.4 all-gather.5
  468.1 106.9 reduce-scatter.8
  645.8 37.4 all-gather.7
  798.3 106.9 reduce-scatter.10
  976.0 37.4 all-gather.9
  1130.8 106.9 reduce-scatter.12
  1310.2 37.4 all-gather.11
  1462.3 106.9 reduce-scatter.14
  1641.7 37.4 all-gather.13
  1796.9 106.9 reduce-scatter.16
where the time goes:
time: 2000 us; the launch traced here: 1980 us
  waiting for transfers between devices  826 us (41%)
  blocking collectives  388 us (19%)
  matrix products  370 us (18%)
  local copies, waits for them, and re-layouts  307 us (15%)
  other arithmetic  50.9 us (3%)
  between operations  23.3 us (1%)
    reduce_scatter x6, waiting for transfers between devices, device_body(): lax.psum_scatter(part_sigma, AXIS_NAME, scatter_dimension=0, tiled=True)  638 us
    dot_general x24, matrix products, term_body(): lax.dot_general(left_loc[term_idx], pair_done, (((1,), (1,)), ((), ())),...  228 us
    psum x6, blocking collectives, device_body(): lax.psum(jnp.sum(residual * residual), AXIS_NAME) / vec_size  196 us
    psum x6, blocking collectives, device_body(): alpha_now = lax.psum(jnp.sum(sigma_slab * current), AXIS_NAME) / vec_size  191 us
    all_gather x5, waiting for transfers between devices, device_body(): lax.all_gather(following.astype(jnp.bfloat16), AXIS_NAME, axis=0, tiled=T...  188 us
    cond x24, local copies, waits for them, and re-layouts, term_body(): lax.cond(flag_loc[term_idx] == 1, apply_right, keep_vector, right_loc[ter...  175 us
    dot_general x24, matrix products, term_body(): lax.dot_general(pair_loc[term_idx], right_done, (((1,), (1,)), ((), ())),...  142 us
    while x6, local copies, waits for them, and re-layouts, local_sigma(): return lax.fori_loop(0, left_loc.shape[0], term_body, start_sum)  77.2 us
  transfers between devices with their start and end apart: 11, of which 11 were waited for; matrix products, arithmetic and copies ran while one was open for 0% of the time, Pallas kernels for 0%

commit v1 on v0

v1 whole, which is shorter than its diff:
```python
import functools

import jax
import jax.numpy as jnp
from jax import lax
from jax.experimental import pallas as pl
from jax.experimental.pallas import tpu as pltpu
from jax.sharding import PartitionSpec as P

STEPS = 6
AXIS = 'terms'
BOND = 384
PAIR = 16
VEC_SIZE = BOND * PAIR * BOND
CHIPS = 8
COLS = BOND // CHIPS
HALF = PAIR // 2
KLOC = 4
CHUNK = 128
NCHUNK = BOND // CHUNK
QROWS = HALF * COLS
ROWS = BOND // 16
MESH = pl.DeviceIdType.MESH
F32 = jnp.float32
BF16 = jnp.bfloat16
PEERS = (1, 2, 4, 3, 5, 6, 7)


def flip(idx, mask, bits):
    out = 0
    for b in range(bits):
        bit = lax.rem(lax.div(idx, 1 << b), 2)
        if (mask >> b) & 1:
            bit = 1 - bit
        out = out + bit * (1 << b)
    return out


def rotl(pos, chunk):
    scaled = pos * (1 + chunk + lax.div(chunk, 2)) if not isinstance(chunk, int) else pos * (1 << chunk)
    return scaled - 7 * lax.div(scaled, 8)


def kernel(u0_ref, v0_ref, l_ref, r_ref, w_ref,
           kry_ref, alpha_ref, beta_ref,
           u, lbuf, rbuf, wbuf, mbuf, ybuf, zbuf, sig, sig_in, wv, vcur, vprev, tbuf, red, beta_prev,
           loc_sem, rs_sem, rr_sem, ws_sem, wr_sem, ls_sem, lr_sem, gs_sem, gr_sem, fs_sem, fr_sem,
           xs_sem, xr_sem, ds_sem, dr_sem, ks_sem, kr_sem, kl_sem):
    me = lax.axis_index(AXIS)
    chip = lax.div(me, 2)
    core = lax.rem(me, 2)
    partner = flip(me, 1, 4)

    def peer(d):
        return flip(chip, d, 3) * 2 + core

    def remote(src, dst, ssem, rsem, dev):
        return pltpu.make_async_remote_copy(src_ref=src, dst_ref=dst, send_sem=ssem, recv_sem=rsem,
                                            device_id=(dev,), device_id_type=MESH)

    local = [pltpu.make_async_copy(l_ref.at[i], lbuf.at[i, pl.ds(0, 512)], loc_sem.at[i]) for i in range(NCHUNK)]
    local.append(pltpu.make_async_copy(u0_ref, u, loc_sem.at[3]))
    local.append(pltpu.make_async_copy(r_ref.at[:, pl.ds(pl.multiple_of(COLS * chip, 16), COLS)], rbuf.at[0], loc_sem.at[4]))
    for c in local:
        c.start()
    barrier = pltpu.get_barrier_semaphore()
    for d in range(1, 16):
        pl.semaphore_signal(barrier, inc=1, device_id=(flip(me, d, 4),), device_id_type=MESH)
    pl.semaphore_wait(barrier, 15)

    w_copies = {d: remote(w_ref, wbuf.at[d], ws_sem.at[d], wr_sem.at[d], peer(d)) for d in PEERS}
    r_copies = {d: remote(r_ref.at[:, pl.ds(pl.multiple_of(COLS * flip(chip, d, 3), 16), COLS)], rbuf.at[d],
                          rs_sem.at[d], rr_sem.at[d], peer(d)) for d in PEERS}

    def l_copy(i, n):
        mask = 1 << ((i + min(n, 2)) % 3)
        src, dst, size = ((0, 512, 512), (0, 1024, 1024), (0, 2048, 1024), (1024, 3072, 1024))[n]
        return remote(lbuf.at[i, pl.ds(src, size)], lbuf.at[i, pl.ds(dst, size)], ls_sem.at[i, n], lr_sem.at[i, n], peer(mask))

    for d in PEERS:
        w_copies[d].start()
    for d in (1, 2, 4):
        r_copies[d].start()
    for i in range(NCHUNK):
        local[i].wait()
        l_copy(i, 0).start()
    for d in (3, 5, 6, 7):
        r_copies[d].start()

    wbuf[0] = w_ref[...]
    for d in PEERS:
        w_copies[d].wait_recv()
    row_id = lax.broadcasted_iota(jnp.int32, (256, 16), 0)
    col_id = lax.broadcasted_iota(jnp.int32, (256, 16), 1)
    spread = jnp.where(lax.div(row_id, 16) == col_id, 1.0, 0.0).astype(BF16)
    row_id = lax.broadcasted_iota(jnp.int32, (128, 256), 0)
    col_id = lax.broadcasted_iota(jnp.int32, (128, 256), 1)
    spread_t = jnp.where(row_id == lax.div(col_id, 16), 1.0, 0.0).astype(BF16)
    row_id = lax.broadcasted_iota(jnp.int32, (256, 256), 0)
    col_id = lax.broadcasted_iota(jnp.int32, (256, 256), 1)
    same = lax.rem(row_id, 16) == lax.rem(col_id, 16)

    def build(slot, carry):
        for k in range(KLOC):
            tall = jnp.dot(spread, wbuf[slot, pl.ds(16 * k, 16), :], preferred_element_type=F32).astype(BF16)
            full = jnp.dot(tall, spread_t, preferred_element_type=F32)
            mbuf[slot * KLOC + k] = jnp.where(same, full, 0.0).astype(BF16)
        return carry

    lax.fori_loop(0, CHIPS, build, 0)

    def group(i, g):
        slot_a = rotl(2 * g, i)
        slot_b = rotl(2 * g + 1, i)
        right = jnp.concatenate([rbuf[slot_a].reshape(KLOC * COLS, BOND), rbuf[slot_b].reshape(KLOC * COLS, BOND)], axis=0)
        for n in range(8):
            lanes = pl.ds(256 * n, 256)
            ybuf[:, lanes] = jnp.dot(right, u[i, :, lanes], preferred_element_type=F32).astype(BF16)
        for kk in range(8):
            mat = mbuf[(slot_a if kk < KLOC else slot_b) * KLOC + kk % KLOC]
            cols = [jnp.concatenate([ybuf[COLS * kk + 16 * t:COLS * kk + 16 * t + 16, 128 * r:128 * r + 128]
                                     for r in range(PAIR)], axis=0) for t in range(3)]
            pair = jnp.dot(mat, jnp.concatenate(cols, axis=1), preferred_element_type=F32).astype(BF16)
            for q in range(PAIR):
                for t in range(3):
                    zbuf[COLS * q + 16 * t:COLS * q + 16 * t + 16, 128 * kk:128 * kk + 128] = \
                        pair[16 * q:16 * q + 16, 128 * t:128 * t + 128]
        left = lbuf[i, pl.ds(pl.multiple_of(g * 1024, 1024), 1024), :]
        sig[...] += jnp.dot(zbuf[...], left, preferred_element_type=F32)

    def all_sum(phase, part):
        red[phase, me] = part
        copies = []
        for d in range(1, 16):
            c = remote(red.at[phase, me], red.at[phase, me], ds_sem.at[phase, d], dr_sem.at[phase, d], flip(me, d, 4))
            c.start()
            copies.append(c)
        for c in copies:
            c.wait_recv()
        total = red[phase, 0]
        for s in range(1, 16):
            total = total + red[phase, s]
        for c in copies:
            c.wait_send()
        return jnp.sum(total, keepdims=True) / VEC_SIZE

    def fold(x):
        out = x[0:8, 0:128]
        for r in range(COLS // 8):
            for c in range(NCHUNK):
                if r or c:
                    out = out + x[8 * r:8 * r + 8, 128 * c:128 * c + 128]
        return out

    def vector_part(j):
        theirs = sig.at[pl.ds(pl.multiple_of(QROWS * (1 - core), QROWS), QROWS)]
        swap = remote(theirs, sig_in, xs_sem, xr_sem, partner)
        swap.start()
        swap.wait_recv()
        part = jnp.zeros((8, 128), F32)
        for q in range(HALF):
            rows = pl.ds(COLS * q, COLS)
            w = sig[pl.ds(pl.multiple_of(QROWS * core + COLS * q, COLS), COLS), :] + sig_in[rows, :]
            wv[rows, :] = w
            part = part + fold(w * vcur[rows, :])
        alpha = all_sum(0, part)
        beta_old = beta_prev[0:1, 0:1]
        part = jnp.zeros((8, 128), F32)
        for q in range(HALF):
            rows = pl.ds(COLS * q, COLS)
            w = wv[rows, :] - alpha * vcur[rows, :] - beta_old * vprev[rows, :]
            wv[rows, :] = w
            part = part + fold(w * w)
        beta = jnp.sqrt(all_sum(1, part))
        for q in range(HALF):
            rows = pl.ds(COLS * q, COLS)
            vprev[rows, :] = vcur[rows, :]
            vcur[rows, :] = wv[rows, :] / beta
        beta_prev[...] = jnp.broadcast_to(beta, (8, 128))
        alpha_ref[j] = jnp.broadcast_to(alpha, (8, 128))
        beta_ref[j] = jnp.broadcast_to(beta, (8, 128))
        swap.wait_send()

    def kry_copies(j):
        return [remote(tbuf.at[pl.ds(pl.multiple_of(ROWS * flip(me, d, 4), 8), ROWS)], kry_ref.at[j, me],
                       ks_sem.at[d], kr_sem.at[d], flip(me, d, 4)) for d in range(1, 16)]

    def kry_own(j):
        return pltpu.make_async_copy(tbuf.at[pl.ds(pl.multiple_of(ROWS * me, 8), ROWS)], kry_ref.at[j, me], kl_sem)

    def kry_start(j):
        tbuf[...] = vcur[...].T
        kry_own(j).start()
        for c in kry_copies(j):
            c.start()

    def kry_wait(j):
        kry_own(j).wait()
        for c in kry_copies(j):
            c.wait()

    vcur[...] = v0_ref[...]
    vprev[...] = jnp.zeros_like(vprev)
    beta_prev[...] = jnp.zeros_like(beta_prev)
    sig[...] = jnp.zeros_like(sig)
    local[3].wait()
    local[4].wait()
    for d in (1, 2, 4):
        r_copies[d].wait_recv()
    for i in range(NCHUNK):
        l_copy(i, 0).wait_recv()
        l_copy(i, 1).start()

    def first_body(idx, carry):
        g = lax.div(idx, 3)
        i = lax.rem(idx, 3)

        @pl.when(idx == 3)
        def _():
            for d in (3, 5, 6, 7):
                r_copies[d].wait_recv()
            for c in range(NCHUNK):
                l_copy(c, 1).wait_recv()
                l_copy(c, 2).start()
            for c in range(NCHUNK):
                l_copy(c, 3).start()

        @pl.when(idx == 6)
        def _():
            for c in range(NCHUNK):
                l_copy(c, 2).wait_recv()

        @pl.when(idx == 9)
        def _():
            for c in range(NCHUNK):
                l_copy(c, 3).wait_recv()

        group(i, g)
        return carry

    lax.fori_loop(0, 12, first_body, 0)
    for d in PEERS:
        w_copies[d].wait_send()
        r_copies[d].wait_send()
    for i in range(NCHUNK):
        for n in range(4):
            l_copy(i, n).wait_send()
    vector_part(0)

    def region(i, c):
        return u.at[i, pl.ds(pl.multiple_of(COLS * c, 16), COLS), pl.ds(pl.multiple_of(HALF * CHUNK * core, 1024), HALF * CHUNK)]

    def gather(i, d):
        return remote(region(i, chip), region(i, chip), gs_sem.at[i, d], gr_sem.at[i, d], peer(d))

    def forward(i, d):
        src = region(i, flip(chip, d, 3))
        return remote(src, src, fs_sem.at[i, d], fr_sem.at[i, d], partner)

    def relay(i):
        for d in PEERS:
            gather(i, d).wait_recv()
            forward(i, d).start()

    def step_body(j, carry):
        for q in range(HALF):
            val = vcur[COLS * q:COLS * q + COLS, :].astype(BF16)
            for i in range(NCHUNK):
                u[i, pl.ds(pl.multiple_of(COLS * chip, 16), COLS),
                  pl.ds(pl.multiple_of(HALF * CHUNK * core + CHUNK * q, 128), CHUNK)] = val[:, CHUNK * i:CHUNK * i + CHUNK]
        for i in range(NCHUNK):
            for d in PEERS:
                gather(i, d).start()
            forward(i, 0).start()
        kry_start(j - 1)
        sig[...] = jnp.zeros_like(sig)
        relay(0)

        def body(idx, carry):
            i = lax.div(idx, 4)
            g = lax.rem(idx, 4)

            for c in range(NCHUNK):
                @pl.when(idx == 4 * c)
                def _():
                    for d in range(8):
                        forward(c, d).wait_recv()
            for c in range(1, NCHUNK):
                @pl.when(idx == 4 * c - 1)
                def _():
                    relay(c)

            group(i, g)
            return carry

        lax.fori_loop(0, 12, body, 0)
        for i in range(NCHUNK):
            forward(i, 0).wait_send()
            for d in PEERS:
                gather(i, d).wait_send()
                forward(i, d).wait_send()
        kry_wait(j - 1)
        vector_part(j)
        return carry

    lax.fori_loop(1, STEPS, step_body, 0)
    kry_start(STEPS - 1)
    kry_wait(STEPS - 1)


def matvec_steps(u0, v0, l_in, r_in, w_in):
    dma = pltpu.SemaphoreType.DMA
    vmem = pl.BlockSpec(memory_space=pltpu.VMEM)
    hbm = pl.BlockSpec(memory_space=pl.ANY)
    return pl.pallas_call(
        kernel,
        out_shape=(jax.ShapeDtypeStruct((STEPS, 16, ROWS, BOND), F32),
                   jax.ShapeDtypeStruct((STEPS, 8, 128), F32),
                   jax.ShapeDtypeStruct((STEPS, 8, 128), F32)),
        in_specs=[hbm, vmem, hbm, hbm, vmem],
        out_specs=(hbm, vmem, vmem),
        scratch_shapes=[
            pltpu.VMEM((NCHUNK, BOND, PAIR * CHUNK), BF16),
            pltpu.VMEM((NCHUNK, CHIPS * KLOC * CHUNK, BOND), BF16),
            pltpu.VMEM((CHIPS, KLOC, COLS, BOND), BF16),
            pltpu.VMEM((CHIPS, KLOC * 16, 128), BF16),
            pltpu.VMEM((CHIPS * KLOC, 256, 256), BF16),
            pltpu.VMEM((2 * KLOC * COLS, PAIR * CHUNK), BF16),
            pltpu.VMEM((PAIR * COLS, 2 * KLOC * CHUNK), BF16),
            pltpu.VMEM((PAIR * COLS, BOND), F32),
            pltpu.VMEM((QROWS, BOND), F32),
            pltpu.VMEM((QROWS, BOND), F32),
            pltpu.VMEM((QROWS, BOND), F32),
            pltpu.VMEM((QROWS, BOND), F32),
            pltpu.VMEM((BOND, QROWS), F32),
            pltpu.VMEM((2, 16, 8, 128), F32),
            pltpu.VMEM((8, 128), F32),
            dma((5,)), dma((8,)), dma((8,)), dma((8,)), dma((8,)),
            dma((NCHUNK, 4)), dma((NCHUNK, 4)),
            dma((NCHUNK, 8)), dma((NCHUNK, 8)), dma((NCHUNK, 8)), dma((NCHUNK, 8)),
            dma, dma, dma((2, 16)), dma((2, 16)), dma((16,)), dma((16,)), dma,
        ],
        compiler_params=pltpu.CompilerParams(collective_id=0, has_side_effects=True, vmem_limit_bytes=60 * 1024 * 1024),
        name='lanczos',
    )(u0, v0, l_in, r_in, w_in)


def solution(mesh):
    def device_body(psi, left_loc, pair_loc, right_loc, flag_loc):
        me = lax.axis_index(AXIS)
        chip, core = me // 2, me % 2
        norm = jnp.sqrt(jnp.sum(psi * psi) / VEC_SIZE)
        first_rows = lax.dynamic_slice_in_dim(psi, me * ROWS, ROWS, axis=0) / norm
        u0 = (psi / norm).astype(BF16).reshape(NCHUNK, CHUNK, PAIR, BOND).transpose(0, 3, 2, 1).reshape(NCHUNK, BOND, PAIR * CHUNK)
        v0 = lax.dynamic_slice(psi, (0, core * HALF, chip * COLS), (BOND, HALF, COLS)) / norm
        v0 = v0.transpose(1, 2, 0).reshape(QROWS, BOND)
        l_in = left_loc.reshape(KLOC, NCHUNK, CHUNK, BOND).transpose(1, 0, 2, 3).reshape(NCHUNK, KLOC * CHUNK, BOND)
        eye = jnp.eye(BOND, dtype=BF16)
        r_in = jnp.where((flag_loc == 1)[:, None, None], right_loc, eye)
        w_in = jnp.pad(pair_loc.reshape(KLOC * PAIR, PAIR), ((0, 0), (0, 128 - PAIR)))
        blocks, alpha, beta = matvec_steps(u0, v0, l_in, r_in, w_in)
        rest = blocks.reshape(STEPS, CHIPS, 2, ROWS, HALF, COLS).transpose(0, 3, 2, 4, 1, 5).reshape(STEPS, ROWS, PAIR, BOND)
        return jnp.concatenate([first_rows[None], rest], axis=0), alpha[:, 0, 0], beta[:, 0, 0]

    return jax.shard_map(device_body, mesh=mesh, in_specs=(P(), P(AXIS), P(AXIS), P(AXIS), P(AXIS)),
                         out_specs=(P(None, AXIS), P(), P()), check_vma=False)
```

time: 2000 us -> 456 us (0.23)
  waiting for transfers between devices: 826 us -> 0 us
  blocking collectives: 388 us -> 0 us
  Pallas kernels: 0 us -> 385 us
  matrix products: 370 us -> 0 us
  local copies, waits for them, and re-layouts: 307 us -> 48.1 us
  other arithmetic: 50.9 us -> 20.5 us
  between operations: 23.3 us -> 1.42 us
    reduce_scatter x6 -> x0, waiting for transfers between devices: 638 us -> none  [device_body(): lax.psum_scatter(part_sigma, AXIS_NAME, scatter_dimension=0, tiled=True)]
    psum x12 -> x0, blocking collectives: 388 us -> none  [the longest x6 196 us: device_body(): lax.psum(jnp.sum(residual * residual), AXIS_NAME) / vec_size]
    pallas_call x0 -> x1, Pallas kernels: none -> 385 us  [matvec_steps(): pl.pallas_call(kernel, out_shape=(jax.ShapeDtypeStruct((STEPS, 16, ROWS,...]
    dot_general x48 -> x0, matrix products: 370 us -> none  [the longest x24 228 us: term_body(): lax.dot_general(left_loc[term_idx], pair_done, (((1,), (1,)), ((), ())),...]
    all_gather x5 -> x0, waiting for transfers between devices: 188 us -> none  [device_body(): lax.all_gather(following.astype(jnp.bfloat16), AXIS_NAME, axis=0, tiled=T...]
    cond x24 -> x0, local copies, waits for them, and re-layouts: 175 us -> none  [term_body(): lax.cond(flag_loc[term_idx] == 1, apply_right, keep_vector, right_loc[ter...]
    while x6 -> x0, local copies, waits for them, and re-layouts: 77.2 us -> none  [local_sigma(): return lax.fori_loop(0, left_loc.shape[0], term_body, start_sum)]
    unnamed x34 -> x8, local copies, waits for them, and re-layouts: 34.4 us -> 0.01 us
  transfers between devices with their start and end apart: 11 -> 0, of which waited for: 11 -> 0; matrix products, arithmetic and copies ran while one was open for 0% -> 0% of each run, Pallas kernels for 0% -> 0%
where the time goes in v1:
time: 456 us; the launch traced here: 455 us
  Pallas kernels  385 us (84%)
  local copies, waits for them, and re-layouts  48.1 us (11%)
  other arithmetic  20.5 us (4%)
    pallas_call x1, Pallas kernels, matvec_steps(): pl.pallas_call(kernel, out_shape=(jax.ShapeDtypeStruct((STEPS, 16, ROWS,...  385 us
    reshape x2, local copies, waits for them, and re-layouts, device_body(): (psi / norm).astype(BF16).reshape(NCHUNK, CHUNK, PAIR, BOND)  15.9 us
    reshape x2, local copies, waits for them, and re-layouts, device_body(): blocks.reshape(STEPS, CHIPS, 2, ROWS, HALF, COLS)  14.9 us
    transpose x1, local copies, waits for them, and re-layouts, device_body(): blocks.reshape(STEPS, CHIPS, 2, ROWS, HALF, COLS)  12.7 us

profile of v1, /device:TPU:0, one launch (start us, length us, event | category | flops | bytes accessed | tf_op | source)
XLA Modules:
  0.0 454.9 jit_solution(7779211555952139424)
XLA Ops:
  0.7 6.7 %multiply_reduce_fusion = f32[]{:T(128)} fusion(f32[384,16,384]{2,1,0:T(8,128)} %param.5), kind=kLoop, calls=%fused_computation.1 | loop fusion | flops 4718591 | bytes 9437188 | tf_op jit(solution)/shard_map/reduce_sum | solution.py:352
  8.1 2.4 divide_bitcast_fusion
  10.4 1.4 copy.13
  11.9 6.6 %divide_convert_fusion = bf16[384,16,384]{2,1,0:T(8,128)(2,1)} fusion(f32[384,16,384]{2,1,0:T(8,128)} %param.5, f32[]{:T(128)S(6)} %sqrt.3), kind=kLoop, calls=%fused_computation | loop fusion | flops 4718592 | bytes 14155780 | tf_op jit(solution)/shard_map/convert_element_type | solution.py:354
  18.4 7.6 %copy.12 = bf16[3,128,16,384]{1,2,3,0:T(8,128)(2,1)} copy(bf16[3,128,16,384]{3,2,1,0:T(8,128)(2,1)} %bitcast.21) | data formatting | bytes 9437184 | tf_op jit(solution)/shard_map/reshape | solution.py:354
  26.0 0.0 copy-start.3
  26.0 0.0 copy-start
  26.0 0.0 copy-start.1
  26.0 8.3 %reshape.32.u0_ref = bf16[3,384,2048]{2,1,0:T(8,128)(2,1)} reshape(bf16[3,384,16,128]{3,2,1,0:T(8,128)(2,1)} %bitcast.20) | data formatting | bytes 9437184 | tf_op jit(solution)/shard_map/reshape | solution.py:354
  34.3 0.0 copy-start.2
  34.4 0.0 copy-done.3
  34.4 0.0 copy-done
  34.4 1.3 broadcast_select_fusion.r_ref
  35.7 0.0 copy-done.1
  35.7 1.2 copy.14
  36.8 0.0 copy-done.2
  36.8 0.6 pad.4.w_ref
  37.4 384.9 %lanczos.1 = (f32[6,16,24,384]{3,2,1,0:T(8,128)}, f32[6,8,128]{2,1,0:T(8,128)}, f32[6,8,128]{2,1,0:T(8,128)}) custom-call(bf16[3,384,2048]{2,1,0:T(8,128)(2,1)} %reshape.32.u0_ref, f32[384,384]{1,0:T(8,128)} %bitcast.23, bf16[3,512,384]{2,1,0:T(8,128)(2,1)} %bitcast.22, bf16[4,384,384]{2,1,0:T(8,128)(2,1)} %broadcast_select_fusion.r_ref, ...), custom_call_target="tpu_custom_call" | custom-call | tf_op jit(solution)/shard_map/lanczos/pallas_call | solution.py:315
  422.4 8.1 %reshape.37 = f32[6,8,2,24,8,48]{5,4,3,2,1,0:T(8,128)} reshape(f32[6,16,24,384]{3,2,1,0:T(8,128)} %get-tuple-element.6) | data formatting | bytes 7077888 | tf_op jit(solution)/shard_map/reshape | solution.py:362
  430.5 12.7 %copy.15 = f32[6,24,2,8,8,48]{5,4,3,2,1,0:T(8,128)} copy(f32[6,24,2,8,8,48]{5,3,1,2,4,0:T(8,128)} %bitcast.19) | data formatting | bytes 7077888 | tf_op jit(solution)/shard_map/transpose | solution.py:362
  443.2 6.7 %reshape.38 = f32[6,24,16,384]{3,2,1,0:T(8,128)S(1)} reshape(f32[6,24,2,8,8,48]{5,4,3,2,1,0:T(8,128)} %copy.15) | data formatting | bytes 7077888 | tf_op jit(solution)/shard_map/reshape | solution.py:362
  450.0 1.1 divide_bitcast_fusion.1
  451.1 2.5 pad_maximum_fusion
  453.5 1.4 slice_reduce_fusion
  (2 shorter events, 0.0 us)
Async XLA Ops:
  26.0 8.4 %copy-start.3 = (s32[4]{0:T(128)S(1)}, s32[4]{0:T(128)}, u32[]{:S(2)}) copy-start(s32[4]{0:T(128)} %param.9) | copy-start | bytes 52
  26.0 8.4 %copy-start = (bf16[4,384,384]{2,1,0:T(8,128)(2,1)S(1)}, bf16[4,384,384]{2,1,0:T(8,128)(2,1)}, u32[]{:S(2)}) copy-start(bf16[4,384,384]{2,1,0:T(8,128)(2,1)} %param.8) | copy-start | bytes 3538948
  26.0 9.7 %copy-start.1 = (bf16[4,384,384]{2,1,0:T(8,128)(2,1)S(1)}, bf16[4,384,384]{2,1,0:T(8,128)(2,1)}, u32[]{:S(2)}) copy-start(bf16[4,384,384]{2,1,0:T(8,128)(2,1)} %param.6) | copy-start | bytes 3538948
  34.3 2.5 copy-start.2

commit v2 on v1

--- a/solution.py
+++ b/solution.py
@@ -1,5 +1,3 @@
-import functools
-
 import jax
 import jax.numpy as jnp
 from jax import lax
@@ -41,10 +39,10 @@
     return scaled - 7 * lax.div(scaled, 8)
 
 
-def kernel(u0_ref, v0_ref, l_ref, r_ref, w_ref,
-           kry_ref, alpha_ref, beta_ref,
-           u, lbuf, rbuf, wbuf, mbuf, ybuf, zbuf, sig, sig_in, wv, vcur, vprev, tbuf, red, beta_prev,
-           loc_sem, rs_sem, rr_sem, ws_sem, wr_sem, ls_sem, lr_sem, gs_sem, gr_sem, fs_sem, fr_sem,
+def kernel(psi_ref, l_ref, r_ref, w_ref,
+           kry_ref, alpha_ref, beta_ref, first_ref,
+           psi, u, lbuf, rbuf, wbuf, mbuf, ybuf, zbuf, sig, sig_in, wv, vcur, vprev, tbuf, red, beta_prev,
+           psi_sem, ll_sem, loc_sem, rs_sem, rr_sem, ws_sem, wr_sem, ls_sem, lr_sem, gs_sem, gr_sem, fs_sem, fr_sem,
            xs_sem, xr_sem, ds_sem, dr_sem, ks_sem, kr_sem, kl_sem):
     me = lax.axis_index(AXIS)
     chip = lax.div(me, 2)
@@ -58,11 +56,20 @@
         return pltpu.make_async_remote_copy(src_ref=src, dst_ref=dst, send_sem=ssem, recv_sem=rsem,
                                             device_id=(dev,), device_id_type=MESH)
 
-    local = [pltpu.make_async_copy(l_ref.at[i], lbuf.at[i, pl.ds(0, 512)], loc_sem.at[i]) for i in range(NCHUNK)]
-    local.append(pltpu.make_async_copy(u0_ref, u, loc_sem.at[3]))
-    local.append(pltpu.make_async_copy(r_ref.at[:, pl.ds(pl.multiple_of(COLS * chip, 16), COLS)], rbuf.at[0], loc_sem.at[4]))
-    for c in local:
-        c.start()
+    l_own = [[pltpu.make_async_copy(l_ref.at[k, pl.ds(CHUNK * i, CHUNK)], lbuf.at[i, pl.ds(CHUNK * k, CHUNK)], ll_sem.at[i, k])
+              for k in range(KLOC)] for i in range(NCHUNK)]
+    r_own = pltpu.make_async_copy(r_ref.at[:, pl.ds(pl.multiple_of(COLS * chip, 16), COLS)], rbuf.at[0], loc_sem)
+    part_rows = BOND * PAIR // 4
+    psi_own = [[pltpu.make_async_copy(psi_ref.at[pl.ds(part_rows * i, part_rows), pl.ds(128 * c, 128)],
+                                      psi.at[c, pl.ds(part_rows * i, part_rows)], psi_sem.at[i, c]) for c in range(3)]
+               for i in range(4)]
+    for i in range(NCHUNK):
+        for k in range(KLOC):
+            l_own[i][k].start()
+    r_own.start()
+    for i in range(4):
+        for c in range(3):
+            psi_own[i][c].start()
     barrier = pltpu.get_barrier_semaphore()
     for d in range(1, 16):
         pl.semaphore_signal(barrier, inc=1, device_id=(flip(me, d, 4),), device_id_type=MESH)
@@ -82,7 +89,8 @@
     for d in (1, 2, 4):
         r_copies[d].start()
     for i in range(NCHUNK):
-        local[i].wait()
+        for k in range(KLOC):
+            l_own[i][k].wait()
         l_copy(i, 0).start()
     for d in (3, 5, 6, 7):
         r_copies[d].start()
@@ -199,12 +207,50 @@
         for c in kry_copies(j):
             c.wait()
 
-    vcur[...] = v0_ref[...]
+    square = jnp.zeros((8, 128), F32)
+    for i in range(4):
+        for c in range(3):
+            psi_own[i][c].wait()
+
+        def add_squares(n, acc, base=i * part_rows):
+            for c in range(3):
+                x = psi[c, pl.ds(pl.multiple_of(base + COLS * n, COLS), COLS), :]
+                x = x * x
+                for r in range(COLS // 8):
+                    acc = acc + x[8 * r:8 * r + 8, :]
+            return acc
+
+        square = lax.fori_loop(0, part_rows // COLS, add_squares, square)
+    norm = jnp.sqrt(jnp.sum(square, keepdims=True) / VEC_SIZE)
+
+    def spread_pair(q, carry):
+        for i in range(NCHUNK):
+            for c in range(NCHUNK):
+                x = psi[c, pl.ds(CHUNK * PAIR * i + q, CHUNK, stride=PAIR), :]
+                x = (x / norm).T
+                u[i, pl.ds(128 * c, 128), pl.ds(pl.multiple_of(CHUNK * q, CHUNK), CHUNK)] = x.astype(BF16)
+                tbuf[pl.ds(128 * c, 128), pl.ds(CHUNK * i, CHUNK)] = x
+
+        @pl.when(lax.div(q, HALF) == core)
+        def _():
+            vcur[pl.ds(pl.multiple_of(COLS * lax.rem(q, HALF), COLS), COLS), :] = tbuf[pl.ds(pl.multiple_of(COLS * chip, COLS), COLS), :]
+
+        return carry
+
+    lax.fori_loop(0, PAIR, spread_pair, 0)
+
+    def first_rows(n, carry):
+        for c in range(3):
+            first_ref[pl.ds(pl.multiple_of(COLS * n, COLS), COLS), pl.ds(128 * c, 128)] = \
+                psi[c, pl.ds(pl.multiple_of(ROWS * PAIR * me + COLS * n, COLS), COLS), :] / norm
+        return carry
+
+    lax.fori_loop(0, ROWS * PAIR // COLS, first_rows, 0)
+
     vprev[...] = jnp.zeros_like(vprev)
     beta_prev[...] = jnp.zeros_like(beta_prev)
     sig[...] = jnp.zeros_like(sig)
-    local[3].wait()
-    local[4].wait()
+    r_own.wait()
     for d in (1, 2, 4):
         r_copies[d].wait_recv()
     for i in range(NCHUNK):
@@ -308,7 +354,7 @@
     kry_wait(STEPS - 1)
 
 
-def matvec_steps(u0, v0, l_in, r_in, w_in):
+def run_steps(psi, left_loc, r_in, w_in):
     dma = pltpu.SemaphoreType.DMA
     vmem = pl.BlockSpec(memory_space=pltpu.VMEM)
     hbm = pl.BlockSpec(memory_space=pl.ANY)
@@ -316,10 +362,12 @@
         kernel,
         out_shape=(jax.ShapeDtypeStruct((STEPS, 16, ROWS, BOND), F32),
                    jax.ShapeDtypeStruct((STEPS, 8, 128), F32),
-                   jax.ShapeDtypeStruct((STEPS, 8, 128), F32)),
-        in_specs=[hbm, vmem, hbm, hbm, vmem],
-        out_specs=(hbm, vmem, vmem),
+                   jax.ShapeDtypeStruct((STEPS, 8, 128), F32),
+                   jax.ShapeDtypeStruct((ROWS * PAIR, BOND), F32)),
+        in_specs=[hbm, hbm, hbm, vmem],
+        out_specs=(hbm, vmem, vmem, vmem),
         scratch_shapes=[
+            pltpu.VMEM((3, BOND * PAIR, 128), F32),
             pltpu.VMEM((NCHUNK, BOND, PAIR * CHUNK), BF16),
             pltpu.VMEM((NCHUNK, CHIPS * KLOC * CHUNK, BOND), BF16),
             pltpu.VMEM((CHIPS, KLOC, COLS, BOND), BF16),
@@ -335,32 +383,50 @@
             pltpu.VMEM((BOND, QROWS), F32),
             pltpu.VMEM((2, 16, 8, 128), F32),
             pltpu.VMEM((8, 128), F32),
-            dma((5,)), dma((8,)), dma((8,)), dma((8,)), dma((8,)),
+            dma((4, 3)), dma((NCHUNK, KLOC)), dma, dma((8,)), dma((8,)), dma((8,)), dma((8,)),
             dma((NCHUNK, 4)), dma((NCHUNK, 4)),
             dma((NCHUNK, 8)), dma((NCHUNK, 8)), dma((NCHUNK, 8)), dma((NCHUNK, 8)),
             dma, dma, dma((2, 16)), dma((2, 16)), dma((16,)), dma((16,)), dma,
         ],
         compiler_params=pltpu.CompilerParams(collective_id=0, has_side_effects=True, vmem_limit_bytes=60 * 1024 * 1024),
         name='lanczos',
-    )(u0, v0, l_in, r_in, w_in)
+    )(psi, left_loc, r_in, w_in)
+
+
+def place_kernel(first_ref, block_ref, out_ref):
+    j = pl.program_id(0)
+
+    @pl.when(j == 0)
+    def _():
+        out_ref[0] = first_ref[...]
+
+    @pl.when(j > 0)
+    def _():
+        for h in range(2):
+            for q in range(HALF):
+                pieces = [block_ref[0, 2 * c + h, :, COLS * q:COLS * q + COLS] for c in range(CHIPS)]
+                out_ref[0, :, HALF * h + q, :] = jnp.concatenate(pieces, axis=1)
+
+
+def place_rows(first, blocks):
+    return pl.pallas_call(
+        place_kernel,
+        grid=(STEPS + 1,),
+        out_shape=jax.ShapeDtypeStruct((STEPS + 1, ROWS, PAIR, BOND), F32),
+        in_specs=[pl.BlockSpec((ROWS, PAIR, BOND), lambda j: (0, 0, 0)),
+                  pl.BlockSpec((1, 16, ROWS, BOND), lambda j: (jnp.maximum(j - 1, 0), 0, 0, 0))],
+        out_specs=pl.BlockSpec((1, ROWS, PAIR, BOND), lambda j: (j, 0, 0, 0)),
+        name='place_rows',
+    )(first, blocks)
 
 
 def solution(mesh):
     def device_body(psi, left_loc, pair_loc, right_loc, flag_loc):
-        me = lax.axis_index(AXIS)
-        chip, core = me // 2, me % 2
-        norm = jnp.sqrt(jnp.sum(psi * psi) / VEC_SIZE)
-        first_rows = lax.dynamic_slice_in_dim(psi, me * ROWS, ROWS, axis=0) / norm
-        u0 = (psi / norm).astype(BF16).reshape(NCHUNK, CHUNK, PAIR, BOND).transpose(0, 3, 2, 1).reshape(NCHUNK, BOND, PAIR * CHUNK)
-        v0 = lax.dynamic_slice(psi, (0, core * HALF, chip * COLS), (BOND, HALF, COLS)) / norm
-        v0 = v0.transpose(1, 2, 0).reshape(QROWS, BOND)
-        l_in = left_loc.reshape(KLOC, NCHUNK, CHUNK, BOND).transpose(1, 0, 2, 3).reshape(NCHUNK, KLOC * CHUNK, BOND)
-        eye = jnp.eye(BOND, dtype=BF16)
-        r_in = jnp.where((flag_loc == 1)[:, None, None], right_loc, eye)
+        r_in = jnp.where((flag_loc == 1)[:, None, None], right_loc, jnp.eye(BOND, dtype=BF16))
         w_in = jnp.pad(pair_loc.reshape(KLOC * PAIR, PAIR), ((0, 0), (0, 128 - PAIR)))
-        blocks, alpha, beta = matvec_steps(u0, v0, l_in, r_in, w_in)
-        rest = blocks.reshape(STEPS, CHIPS, 2, ROWS, HALF, COLS).transpose(0, 3, 2, 4, 1, 5).reshape(STEPS, ROWS, PAIR, BOND)
-        return jnp.concatenate([first_rows[None], rest], axis=0), alpha[:, 0, 0], beta[:, 0, 0]
+        blocks, alpha, beta, first = run_steps(psi.reshape(BOND * PAIR, BOND), left_loc, r_in, w_in)
+        krylov = place_rows(first.reshape(ROWS, PAIR, BOND), blocks)
+        return krylov, alpha[:, 0, 0], beta[:, 0, 0]
 
     return jax.shard_map(device_body, mesh=mesh, in_specs=(P(), P(AXIS), P(AXIS), P(AXIS), P(AXIS)),
                          out_specs=(P(None, AXIS), P(), P()), check_vma=False)

time: 456 us -> 400 us (0.88)
  local copies, waits for them, and re-layouts: 48.1 us -> 2 us
  other arithmetic: 20.5 us -> 3.21 us
  Pallas kernels: 385 us -> 394 us
    reshape x5 -> x0, local copies, waits for them, and re-layouts: 31.9 us -> none  [the longest x2 15.9 us: device_body(): (psi / norm).astype(BF16).reshape(NCHUNK, CHUNK, PAIR, BOND)]
    transpose x2 -> x0, local copies, waits for them, and re-layouts: 14.1 us -> none  [the longest x1 12.7 us: device_body(): blocks.reshape(STEPS, CHIPS, 2, ROWS, HALF, COLS)]
    pallas_call x1 -> x2, Pallas kernels: 385 us -> 394 us  [the longest x1 386 us: run_steps(): pl.pallas_call(kernel, out_shape=(jax.ShapeDtypeStruct((STEPS, 16, ROWS,...]
    reduce_sum x1 -> x0, other arithmetic: 6.71 us -> none  [device_body(): norm = jnp.sqrt(jnp.sum(psi * psi) / VEC_SIZE)]
    convert_element_type x2 -> x1, other arithmetic: 6.58 us -> 0.03 us  [device_body(): jnp.eye(BOND, dtype=BF16)]
where the time goes in v2:
time: 400 us
  Pallas kernels  394 us (98%)
    pallas_call x1, Pallas kernels, run_steps(): pl.pallas_call(kernel, out_shape=(jax.ShapeDtypeStruct((STEPS, 16, ROWS,...  386 us

profile of v2, /device:TPU:0, one launch (start us, length us, event | category | flops | bytes accessed | tf_op | source)
XLA Modules:
  0.0 399.6 jit_solution(10251801736702231456)
XLA Ops:
  0.7 0.7 broadcast_compare_fusion
  1.3 0.0 copy-start
  1.3 2.5 broadcast_select_fusion.r_ref
  3.9 0.0 copy-done
  3.9 0.6 pad.4.w_ref
  4.5 386.0 %lanczos.1 = (f32[6,16,24,384]{3,2,1,0:T(8,128)}, f32[6,8,128]{2,1,0:T(8,128)}, f32[6,8,128]{2,1,0:T(8,128)}, f32[384,384]{1,0:T(8,128)}) custom-call(f32[6144,384]{1,0:T(8,128)} %bitcast.3, bf16[4,384,384]{2,1,0:T(8,128)(2,1)} %l_ref.1, bf16[4,384,384]{2,1,0:T(8,128)(2,1)} %broadcast_select_fusion.r_ref, bf16[64,128]{1,0:T(8,128)(2,1)} %pad.4.w_ref), custom_call_target="tpu_custom_call" | custom-call | tf_op jit(solution)/shard_map/lanczos/pallas_call | solution.py:361
  390.5 1.4 slice_reduce_fusion
  391.9 7.8 %place_rows.1 = f32[7,24,16,384]{3,2,1,0:T(8,128)} custom-call(f32[24,16,384]{2,1,0:T(8,128)} %bitcast.4, f32[6,16,24,384]{3,2,1,0:T(8,128)} %get-tuple-element.8.block_ref), custom_call_target="tpu_custom_call" | custom-call | tf_op jit(solution)/shard_map/place_rows/pallas_call | solution.py:412
  (1 shorter events, 0.0 us)
Async XLA Ops:
  1.3 2.5 copy-start

commit v3 on v2

--- a/solution.py
+++ b/solution.py
@@ -22,6 +22,7 @@
 F32 = jnp.float32
 BF16 = jnp.bfloat16
 PEERS = (1, 2, 4, 3, 5, 6, 7)
+FORWARD_AT = 3
 
 
 def flip(idx, mask, bits):
@@ -41,7 +42,7 @@
 
 def kernel(psi_ref, l_ref, r_ref, w_ref,
            kry_ref, alpha_ref, beta_ref, first_ref,
-           psi, u, lbuf, rbuf, wbuf, mbuf, ybuf, zbuf, sig, sig_in, wv, vcur, vprev, tbuf, red, beta_prev,
+           psi, u, lbuf, rbuf, wbuf, mbuf, ya, yb, z, sig, sig_in, wv, vcur, vprev, red, norm_v, delta_now, beta_now,
            psi_sem, ll_sem, loc_sem, rs_sem, rr_sem, ws_sem, wr_sem, ls_sem, lr_sem, gs_sem, gr_sem, fs_sem, fr_sem,
            xs_sem, xr_sem, ds_sem, dr_sem, ks_sem, kr_sem, kl_sem):
     me = lax.axis_index(AXIS)
@@ -56,7 +57,7 @@
         return pltpu.make_async_remote_copy(src_ref=src, dst_ref=dst, send_sem=ssem, recv_sem=rsem,
                                             device_id=(dev,), device_id_type=MESH)
 
-    l_own = [[pltpu.make_async_copy(l_ref.at[k, pl.ds(CHUNK * i, CHUNK)], lbuf.at[i, pl.ds(CHUNK * k, CHUNK)], ll_sem.at[i, k])
+    l_own = [[pltpu.make_async_copy(l_ref.at[k, :, pl.ds(CHUNK * i, CHUNK)], lbuf.at[i, :, pl.ds(CHUNK * k, CHUNK)], ll_sem.at[i, k])
               for k in range(KLOC)] for i in range(NCHUNK)]
     r_own = pltpu.make_async_copy(r_ref.at[:, pl.ds(pl.multiple_of(COLS * chip, 16), COLS)], rbuf.at[0], loc_sem)
     part_rows = BOND * PAIR // 4
@@ -79,10 +80,20 @@
     r_copies = {d: remote(r_ref.at[:, pl.ds(pl.multiple_of(COLS * flip(chip, d, 3), 16), COLS)], rbuf.at[d],
                           rs_sem.at[d], rr_sem.at[d], peer(d)) for d in PEERS}
 
-    def l_copy(i, n):
+    def l_copies(i, n):
         mask = 1 << ((i + min(n, 2)) % 3)
         src, dst, size = ((0, 512, 512), (0, 1024, 1024), (0, 2048, 1024), (1024, 3072, 1024))[n]
-        return remote(lbuf.at[i, pl.ds(src, size)], lbuf.at[i, pl.ds(dst, size)], ls_sem.at[i, n], lr_sem.at[i, n], peer(mask))
+        spans = ((CHUNK * i, 2 * CHUNK),) if i < 2 else ((2 * CHUNK, CHUNK), (0, CHUNK))
+        return [remote(lbuf.at[i, pl.ds(row, num), pl.ds(src, size)], lbuf.at[i, pl.ds(row, num), pl.ds(dst, size)],
+                       ls_sem.at[i, n, m], lr_sem.at[i, n, m], peer(mask)) for m, (row, num) in enumerate(spans)]
+
+    def l_start(i, n):
+        for c in l_copies(i, n):
+            c.start()
+
+    def l_wait(i, n):
+        for c in l_copies(i, n):
+            c.wait_recv()
 
     for d in PEERS:
         w_copies[d].start()
@@ -91,7 +102,7 @@
     for i in range(NCHUNK):
         for k in range(KLOC):
             l_own[i][k].wait()
-        l_copy(i, 0).start()
+        l_start(i, 0)
     for d in (3, 5, 6, 7):
         r_copies[d].start()
 
@@ -117,40 +128,30 @@
 
     lax.fori_loop(0, CHIPS, build, 0)
 
-    def group(i, g):
+    def right_part(i, g, y):
         slot_a = rotl(2 * g, i)
         slot_b = rotl(2 * g + 1, i)
         right = jnp.concatenate([rbuf[slot_a].reshape(KLOC * COLS, BOND), rbuf[slot_b].reshape(KLOC * COLS, BOND)], axis=0)
         for n in range(8):
             lanes = pl.ds(256 * n, 256)
-            ybuf[:, lanes] = jnp.dot(right, u[i, :, lanes], preferred_element_type=F32).astype(BF16)
+            y[:, lanes] = jnp.dot(right, u[i, :, lanes], preferred_element_type=F32).astype(BF16)
+
+    def pair_part(i, g, y, slot):
+        slot_a = rotl(2 * g, i)
+        slot_b = rotl(2 * g + 1, i)
         for kk in range(8):
             mat = mbuf[(slot_a if kk < KLOC else slot_b) * KLOC + kk % KLOC]
-            cols = [jnp.concatenate([ybuf[COLS * kk + 16 * t:COLS * kk + 16 * t + 16, 128 * r:128 * r + 128]
+            cols = [jnp.concatenate([y[COLS * kk + 16 * t:COLS * kk + 16 * t + 16, 128 * r:128 * r + 128]
                                      for r in range(PAIR)], axis=0) for t in range(3)]
             pair = jnp.dot(mat, jnp.concatenate(cols, axis=1), preferred_element_type=F32).astype(BF16)
             for q in range(PAIR):
                 for t in range(3):
-                    zbuf[COLS * q + 16 * t:COLS * q + 16 * t + 16, 128 * kk:128 * kk + 128] = \
+                    z[slot, COLS * q + 16 * t:COLS * q + 16 * t + 16, 128 * kk:128 * kk + 128] = \
                         pair[16 * q:16 * q + 16, 128 * t:128 * t + 128]
-        left = lbuf[i, pl.ds(pl.multiple_of(g * 1024, 1024), 1024), :]
-        sig[...] += jnp.dot(zbuf[...], left, preferred_element_type=F32)
-
-    def all_sum(phase, part):
-        red[phase, me] = part
-        copies = []
-        for d in range(1, 16):
-            c = remote(red.at[phase, me], red.at[phase, me], ds_sem.at[phase, d], dr_sem.at[phase, d], flip(me, d, 4))
-            c.start()
-            copies.append(c)
-        for c in copies:
-            c.wait_recv()
-        total = red[phase, 0]
-        for s in range(1, 16):
-            total = total + red[phase, s]
-        for c in copies:
-            c.wait_send()
-        return jnp.sum(total, keepdims=True) / VEC_SIZE
+
+    def left_part(i, g, slot):
+        left = lbuf[i, :, pl.ds(pl.multiple_of(g * 1024, 1024), 1024)]
+        sig[...] += lax.dot_general(left, z[slot], (((1,), (1,)), ((), ())), preferred_element_type=F32)
 
     def fold(x):
         out = x[0:8, 0:128]
@@ -160,44 +161,87 @@
                     out = out + x[8 * r:8 * r + 8, 128 * c:128 * c + 128]
         return out
 
+    def total(x):
+        return jnp.sum(x, keepdims=True)
+
     def vector_part(j):
-        theirs = sig.at[pl.ds(pl.multiple_of(QROWS * (1 - core), QROWS), QROWS)]
-        swap = remote(theirs, sig_in, xs_sem, xr_sem, partner)
+        lanes = pl.ds(pl.multiple_of(QROWS * core, 128), QROWS)
+        swap = remote(sig.at[:, pl.ds(pl.multiple_of(QROWS * (1 - core), 128), QROWS)], sig_in, xs_sem, xr_sem, partner)
         swap.start()
+        beta_old = beta_now[0:1, 0:1]
         swap.wait_recv()
-        part = jnp.zeros((8, 128), F32)
-        for q in range(HALF):
-            rows = pl.ds(COLS * q, COLS)
-            w = sig[pl.ds(pl.multiple_of(QROWS * core + COLS * q, COLS), COLS), :] + sig_in[rows, :]
+        s_wv = jnp.zeros((8, 128), F32)
+        s_cv = jnp.zeros((8, 128), F32)
+        for n in range(BOND // COLS):
+            rows = pl.ds(COLS * n, COLS)
+            w = sig[rows, lanes] + sig_in[rows, :]
+            v = vcur[rows, :]
+            s_wv = s_wv + fold(w * v)
+            w = w - beta_old * vprev[rows, :]
+            s_cv = s_cv + fold(w * v)
             wv[rows, :] = w
-            part = part + fold(w * vcur[rows, :])
-        alpha = all_sum(0, part)
-        beta_old = beta_prev[0:1, 0:1]
-        part = jnp.zeros((8, 128), F32)
-        for q in range(HALF):
-            rows = pl.ds(COLS * q, COLS)
-            w = wv[rows, :] - alpha * vcur[rows, :] - beta_old * vprev[rows, :]
+        s_vv = total(norm_v[...])
+        guess = jnp.where(s_vv > 0.0, total(s_cv) / jnp.where(s_vv > 0.0, s_vv, 1.0), 0.0)
+        s_ww = jnp.zeros((8, 128), F32)
+        s_w2v = jnp.zeros((8, 128), F32)
+        for n in range(BOND // COLS):
+            rows = pl.ds(COLS * n, COLS)
+            v = vcur[rows, :]
+            w = wv[rows, :] - guess * v
             wv[rows, :] = w
-            part = part + fold(w * w)
-        beta = jnp.sqrt(all_sum(1, part))
-        for q in range(HALF):
-            rows = pl.ds(COLS * q, COLS)
-            vprev[rows, :] = vcur[rows, :]
-            vcur[rows, :] = wv[rows, :] / beta
-        beta_prev[...] = jnp.broadcast_to(beta, (8, 128))
+            s_ww = s_ww + fold(w * w)
+            s_w2v = s_w2v + fold(w * v)
+        row_of = lax.broadcasted_iota(jnp.int32, (8, 128), 0)
+        message = jnp.where(row_of == 0, total(s_wv),
+                            jnp.where(row_of == 1, guess,
+                                      jnp.where(row_of == 2, s_vv, jnp.where(row_of == 3, total(s_ww), total(s_w2v)))))
+        phase = lax.rem(j, 2)
+        mine = pl.ds(pl.multiple_of(8 * me, 8), 8)
+        red[phase, mine, :] = message
+        copies = [remote(red.at[phase, mine], red.at[phase, mine], ds_sem.at[phase, d], dr_sem.at[phase, d], flip(me, d, 4))
+                  for d in range(1, 16)]
+        for c in copies:
+            c.start()
+        for c in copies:
+            c.wait_recv()
+        table = red.at[phase]
+        a_wv, a_guess, a_vv, a_ww, a_w2v = [table[pl.ds(r, 16, stride=8), :] for r in range(5)]
+        alpha = jnp.sum(a_wv, axis=0, keepdims=True) / VEC_SIZE
+        shift = alpha - a_guess
+        beta = jnp.sqrt(jnp.sum(a_ww - 2.0 * shift * a_w2v + shift * shift * a_vv, axis=0, keepdims=True) / VEC_SIZE)
+        beta_now[...] = jnp.broadcast_to(beta, (8, 128))
+        delta_now[...] = jnp.broadcast_to(alpha[0:1, 0:1] - guess, (8, 128))
         alpha_ref[j] = jnp.broadcast_to(alpha, (8, 128))
         beta_ref[j] = jnp.broadcast_to(beta, (8, 128))
+        norm_v[...] = jnp.zeros_like(norm_v)
+        for c in copies:
+            c.wait_send()
         swap.wait_send()
 
+    def advance(i):
+        beta = beta_now[0:1, 0:1]
+        delta = delta_now[0:1, 0:1]
+        rows = pl.ds(CHUNK * i, CHUNK)
+        old = vcur[rows, :]
+        new = (wv[rows, :] - delta * old) / beta
+        vprev[rows, :] = old
+        vcur[rows, :] = new
+        square = new * new
+        acc = norm_v[...]
+        for r in range(CHUNK // 8):
+            for c in range(NCHUNK):
+                acc = acc + square[8 * r:8 * r + 8, 128 * c:128 * c + 128]
+        norm_v[...] = acc
+        return new
+
     def kry_copies(j):
-        return [remote(tbuf.at[pl.ds(pl.multiple_of(ROWS * flip(me, d, 4), 8), ROWS)], kry_ref.at[j, me],
+        return [remote(vcur.at[pl.ds(pl.multiple_of(ROWS * flip(me, d, 4), 8), ROWS)], kry_ref.at[j, me],
                        ks_sem.at[d], kr_sem.at[d], flip(me, d, 4)) for d in range(1, 16)]
 
     def kry_own(j):
-        return pltpu.make_async_copy(tbuf.at[pl.ds(pl.multiple_of(ROWS * me, 8), ROWS)], kry_ref.at[j, me], kl_sem)
+        return pltpu.make_async_copy(vcur.at[pl.ds(pl.multiple_of(ROWS * me, 8), ROWS)], kry_ref.at[j, me], kl_sem)
 
     def kry_start(j):
-        tbuf[...] = vcur[...].T
         kry_own(j).start()
         for c in kry_copies(j):
             c.start()
@@ -229,15 +273,24 @@
                 x = psi[c, pl.ds(CHUNK * PAIR * i + q, CHUNK, stride=PAIR), :]
                 x = (x / norm).T
                 u[i, pl.ds(128 * c, 128), pl.ds(pl.multiple_of(CHUNK * q, CHUNK), CHUNK)] = x.astype(BF16)
-                tbuf[pl.ds(128 * c, 128), pl.ds(CHUNK * i, CHUNK)] = x
+                wv[pl.ds(128 * c, 128), pl.ds(CHUNK * i, CHUNK)] = x
 
         @pl.when(lax.div(q, HALF) == core)
         def _():
-            vcur[pl.ds(pl.multiple_of(COLS * lax.rem(q, HALF), COLS), COLS), :] = tbuf[pl.ds(pl.multiple_of(COLS * chip, COLS), COLS), :]
+            sig[pl.ds(pl.multiple_of(COLS * lax.rem(q, HALF), COLS), COLS), 0:BOND] = wv[pl.ds(pl.multiple_of(COLS * chip, COLS), COLS), :]
 
         return carry
 
     lax.fori_loop(0, PAIR, spread_pair, 0)
+    start = jnp.zeros((8, 128), F32)
+    for i in range(NCHUNK):
+        x = sig[:, pl.ds(CHUNK * i, CHUNK)].T
+        vcur[pl.ds(CHUNK * i, CHUNK), :] = x
+        x = x * x
+        for r in range(CHUNK // 8):
+            for c in range(NCHUNK):
+                start = start + x[8 * r:8 * r + 8, 128 * c:128 * c + 128]
+    norm_v[...] = start
 
     def first_rows(n, carry):
         for c in range(3):
@@ -248,49 +301,68 @@
     lax.fori_loop(0, ROWS * PAIR // COLS, first_rows, 0)
 
     vprev[...] = jnp.zeros_like(vprev)
-    beta_prev[...] = jnp.zeros_like(beta_prev)
+    beta_now[...] = jnp.zeros_like(beta_now)
     sig[...] = jnp.zeros_like(sig)
     r_own.wait()
-    for d in (1, 2, 4):
+    for i in range(NCHUNK):
+        l_wait(i, 0)
+        l_start(i, 1)
+    for d in PEERS:
         r_copies[d].wait_recv()
-    for i in range(NCHUNK):
-        l_copy(i, 0).wait_recv()
-        l_copy(i, 1).start()
-
-    def first_body(idx, carry):
-        g = lax.div(idx, 3)
-        i = lax.rem(idx, 3)
-
-        @pl.when(idx == 3)
+
+    def front_body(n, carry):
+        @pl.when(n == FORWARD_AT)
         def _():
-            for d in (3, 5, 6, 7):
-                r_copies[d].wait_recv()
-            for c in range(NCHUNK):
-                l_copy(c, 1).wait_recv()
-                l_copy(c, 2).start()
-            for c in range(NCHUNK):
-                l_copy(c, 3).start()
-
-        @pl.when(idx == 6)
-        def _():
-            for c in range(NCHUNK):
-                l_copy(c, 2).wait_recv()
-
-        @pl.when(idx == 9)
-        def _():
-            for c in range(NCHUNK):
-                l_copy(c, 3).wait_recv()
-
-        group(i, g)
+            for i in range(NCHUNK):
+                l_wait(i, 1)
+                l_start(i, 2)
+            for i in range(NCHUNK):
+                l_start(i, 3)
+
+        i = lax.div(n, 2)
+        g = 2 * lax.rem(n, 2)
+        right_part(i, g, ya)
+        right_part(i, g + 1, yb)
+        pair_part(i, g, ya, 4 * i + g)
+        pair_part(i, g + 1, yb, 4 * i + g + 1)
         return carry
 
-    lax.fori_loop(0, 12, first_body, 0)
+    lax.fori_loop(0, 6, front_body, 0)
+
+    def mirror(i, g):
+        other = lax.rem(i + 2, 3)
+        for k in range(2):
+            slot = rotl(2 * g + k, i)
+            pos = rotl(slot, lax.rem(3 - other, 3))
+            for n in range(KLOC):
+                block = lbuf[other, pl.ds(pl.multiple_of(CHUNK * i, CHUNK), CHUNK),
+                             pl.ds(pl.multiple_of(CHUNK * (KLOC * pos + n), CHUNK), CHUNK)]
+                lbuf[i, pl.ds(pl.multiple_of(CHUNK * other, CHUNK), CHUNK),
+                     pl.ds(pl.multiple_of(CHUNK * (KLOC * (2 * g + k) + n), CHUNK), CHUNK)] = block.T
+
+    def back(g):
+        def body(i, carry):
+            mirror(i, g)
+            left_part(i, g, 4 * i + g)
+            return carry
+
+        lax.fori_loop(0, NCHUNK, body, 0)
+
+    back(0)
+    for i in range(NCHUNK):
+        l_wait(i, 2)
+    back(2)
+    for i in range(NCHUNK):
+        l_wait(i, 3)
+    back(1)
+    back(3)
     for d in PEERS:
         w_copies[d].wait_send()
         r_copies[d].wait_send()
     for i in range(NCHUNK):
         for n in range(4):
-            l_copy(i, n).wait_send()
+            for c in l_copies(i, n):
+                c.wait_send()
     vector_part(0)
 
     def region(i, c):
@@ -309,12 +381,11 @@
             forward(i, d).start()
 
     def step_body(j, carry):
-        for q in range(HALF):
-            val = vcur[COLS * q:COLS * q + COLS, :].astype(BF16)
-            for i in range(NCHUNK):
+        for i in range(NCHUNK):
+            flat = advance(i).astype(BF16).T
+            for q in range(HALF):
                 u[i, pl.ds(pl.multiple_of(COLS * chip, 16), COLS),
-                  pl.ds(pl.multiple_of(HALF * CHUNK * core + CHUNK * q, 128), CHUNK)] = val[:, CHUNK * i:CHUNK * i + CHUNK]
-        for i in range(NCHUNK):
+                  pl.ds(pl.multiple_of(HALF * CHUNK * core + CHUNK * q, 128), CHUNK)] = flat[COLS * q:COLS * q + COLS, :]
             for d in PEERS:
                 gather(i, d).start()
             forward(i, 0).start()
@@ -322,24 +393,29 @@
         sig[...] = jnp.zeros_like(sig)
         relay(0)
 
-        def body(idx, carry):
-            i = lax.div(idx, 4)
-            g = lax.rem(idx, 4)
+        def body(n, carry):
+            i = lax.div(n, 2)
+            g = 2 * lax.rem(n, 2)
 
             for c in range(NCHUNK):
-                @pl.when(idx == 4 * c)
+                @pl.when(n == 2 * c)
                 def _():
                     for d in range(8):
                         forward(c, d).wait_recv()
             for c in range(1, NCHUNK):
-                @pl.when(idx == 4 * c - 1)
+                @pl.when(n == 2 * c - 1)
                 def _():
                     relay(c)
 
-            group(i, g)
+            right_part(i, g, ya)
+            right_part(i, g + 1, yb)
+            pair_part(i, g, ya, 0)
+            left_part(i, g, 0)
+            pair_part(i, g + 1, yb, 1)
+            left_part(i, g + 1, 1)
             return carry
 
-        lax.fori_loop(0, 12, body, 0)
+        lax.fori_loop(0, 6, body, 0)
         for i in range(NCHUNK):
             forward(i, 0).wait_send()
             for d in PEERS:
@@ -350,6 +426,8 @@
         return carry
 
     lax.fori_loop(1, STEPS, step_body, 0)
+    for i in range(NCHUNK):
+        advance(i)
     kry_start(STEPS - 1)
     kry_wait(STEPS - 1)
 
@@ -369,22 +447,24 @@
         scratch_shapes=[
             pltpu.VMEM((3, BOND * PAIR, 128), F32),
             pltpu.VMEM((NCHUNK, BOND, PAIR * CHUNK), BF16),
-            pltpu.VMEM((NCHUNK, CHIPS * KLOC * CHUNK, BOND), BF16),
+            pltpu.VMEM((NCHUNK, BOND, CHIPS * KLOC * CHUNK), BF16),
             pltpu.VMEM((CHIPS, KLOC, COLS, BOND), BF16),
             pltpu.VMEM((CHIPS, KLOC * 16, 128), BF16),
             pltpu.VMEM((CHIPS * KLOC, 256, 256), BF16),
             pltpu.VMEM((2 * KLOC * COLS, PAIR * CHUNK), BF16),
-            pltpu.VMEM((PAIR * COLS, 2 * KLOC * CHUNK), BF16),
-            pltpu.VMEM((PAIR * COLS, BOND), F32),
-            pltpu.VMEM((QROWS, BOND), F32),
-            pltpu.VMEM((QROWS, BOND), F32),
-            pltpu.VMEM((QROWS, BOND), F32),
-            pltpu.VMEM((QROWS, BOND), F32),
+            pltpu.VMEM((2 * KLOC * COLS, PAIR * CHUNK), BF16),
+            pltpu.VMEM((12, PAIR * COLS, 2 * KLOC * CHUNK), BF16),
+            pltpu.VMEM((BOND, PAIR * COLS), F32),
             pltpu.VMEM((BOND, QROWS), F32),
-            pltpu.VMEM((2, 16, 8, 128), F32),
+            pltpu.VMEM((BOND, QROWS), F32),
+            pltpu.VMEM((BOND, QROWS), F32),
+            pltpu.VMEM((BOND, QROWS), F32),
+            pltpu.VMEM((2, 16 * 8, 128), F32),
+            pltpu.VMEM((8, 128), F32),
+            pltpu.VMEM((8, 128), F32),
             pltpu.VMEM((8, 128), F32),
             dma((4, 3)), dma((NCHUNK, KLOC)), dma, dma((8,)), dma((8,)), dma((8,)), dma((8,)),
-            dma((NCHUNK, 4)), dma((NCHUNK, 4)),
+            dma((NCHUNK, 4, 2)), dma((NCHUNK, 4, 2)),
             dma((NCHUNK, 8)), dma((NCHUNK, 8)), dma((NCHUNK, 8)), dma((NCHUNK, 8)),
             dma, dma, dma((2, 16)), dma((2, 16)), dma((16,)), dma((16,)), dma,
         ],

time: 400 us -> 355 us (0.89)
  Pallas kernels: 394 us -> 348 us
    pallas_call x1, Pallas kernels: 386 us -> 341 us  [run_steps(): pl.pallas_call(kernel, out_shape=(jax.ShapeDtypeStruct((STEPS, 16, ROWS,...]
where the time goes in v3:
time: 355 us; the launch traced here: 354 us
  Pallas kernels  348 us (98%)
    pallas_call x1, Pallas kernels, run_steps(): pl.pallas_call(kernel, out_shape=(jax.ShapeDtypeStruct((STEPS, 16, ROWS,...  341 us
    pallas_call x1, Pallas kernels, place_rows(): pl.pallas_call(place_kernel, grid=(STEPS + 1,), out_shape=jax.ShapeDtypeS...  7.76 us

profile of v3, /device:TPU:0, one launch (start us, length us, event | category | flops | bytes accessed | tf_op | source)
XLA Modules:
  0.0 354.2 jit_solution(13621308014895737283)
XLA Ops:
  0.7 0.7 broadcast_compare_fusion
  1.3 0.0 copy-start
  1.3 2.5 broadcast_select_fusion.r_ref
  3.9 0.0 copy-done
  3.9 0.6 pad.4.w_ref
  4.5 340.6 %lanczos.1 = (f32[6,16,24,384]{3,2,1,0:T(8,128)}, f32[6,8,128]{2,1,0:T(8,128)}, f32[6,8,128]{2,1,0:T(8,128)}, f32[384,384]{1,0:T(8,128)}) custom-call(f32[6144,384]{1,0:T(8,128)} %bitcast.3, bf16[4,384,384]{2,1,0:T(8,128)(2,1)} %l_ref.1, bf16[4,384,384]{2,1,0:T(8,128)(2,1)} %broadcast_select_fusion.r_ref, bf16[64,128]{1,0:T(8,128)(2,1)} %pad.4.w_ref), custom_call_target="tpu_custom_call" | custom-call | tf_op jit(solution)/shard_map/lanczos/pallas_call | solution.py:439
  345.0 1.4 slice_reduce_fusion
  346.4 7.8 %place_rows.1 = f32[7,24,16,384]{3,2,1,0:T(8,128)} custom-call(f32[24,16,384]{2,1,0:T(8,128)} %bitcast.4, f32[6,16,24,384]{3,2,1,0:T(8,128)} %get-tuple-element.8.block_ref), custom_call_target="tpu_custom_call" | custom-call | tf_op jit(solution)/shard_map/place_rows/pallas_call | solution.py:492
  (1 shorter events, 0.0 us)
Async XLA Ops:
  1.3 2.5 copy-start

commit v4 on v3

--- a/solution.py
+++ b/solution.py
@@ -365,20 +365,44 @@
                 c.wait_send()
     vector_part(0)
 
-    def region(i, c):
-        return u.at[i, pl.ds(pl.multiple_of(COLS * c, 16), COLS), pl.ds(pl.multiple_of(HALF * CHUNK * core, 1024), HALF * CHUNK)]
-
-    def gather(i, d):
-        return remote(region(i, chip), region(i, chip), gs_sem.at[i, d], gr_sem.at[i, d], peer(d))
-
-    def forward(i, d):
-        src = region(i, flip(chip, d, 3))
-        return remote(src, src, fs_sem.at[i, d], fr_sem.at[i, d], partner)
-
-    def relay(i):
-        for d in PEERS:
-            gather(i, d).wait_recv()
-            forward(i, d).start()
+    def region(i, c, r):
+        return u.at[i, pl.ds(pl.multiple_of(COLS * c + 16 * r, 16), 16), pl.ds(pl.multiple_of(HALF * CHUNK * core, 1024), HALF * CHUNK)]
+
+    def axis_of(r, ph):
+        return 1 << ((r + ph) % 3)
+
+    def masks(r, ph):
+        out = [0]
+        for n in range(ph):
+            out += [m ^ axis_of(r, n) for m in out]
+        return out
+
+    def tree(i, ph, r):
+        out = []
+        for n, m in enumerate(masks(r, ph)):
+            src = region(i, flip(chip, m, 3), r)
+            num = (1 << ph) - 1 + n
+            out.append(remote(src, src, gs_sem.at[i, r, num], gr_sem.at[i, r, num], peer(axis_of(r, ph))))
+        return out
+
+    def forward(i, r, m):
+        src = region(i, flip(chip, m, 3), r)
+        return remote(src, src, fs_sem.at[i, r, m], fr_sem.at[i, r, m], partner)
+
+    def tree_start(i, ph):
+        for r in range(3):
+            for c in tree(i, ph, r):
+                c.start()
+
+    def tree_next(i, ph):
+        for r in range(3):
+            for c in tree(i, ph, r):
+                c.wait_recv()
+            if ph < 2:
+                for c in tree(i, ph + 1, r):
+                    c.start()
+            for m in masks(r, ph):
+                forward(i, r, m ^ axis_of(r, ph)).start()
 
     def step_body(j, carry):
         for i in range(NCHUNK):
@@ -386,26 +410,37 @@
             for q in range(HALF):
                 u[i, pl.ds(pl.multiple_of(COLS * chip, 16), COLS),
                   pl.ds(pl.multiple_of(HALF * CHUNK * core + CHUNK * q, 128), CHUNK)] = flat[COLS * q:COLS * q + COLS, :]
-            for d in PEERS:
-                gather(i, d).start()
-            forward(i, 0).start()
-        kry_start(j - 1)
+            tree_start(i, 0)
+            for r in range(3):
+                forward(i, r, 0).start()
         sig[...] = jnp.zeros_like(sig)
-        relay(0)
+        tree_next(0, 0)
+        tree_next(1, 0)
+        tree_next(0, 1)
+        tree_next(1, 1)
+        tree_next(2, 0)
+        tree_next(0, 2)
 
         def body(n, carry):
             i = lax.div(n, 2)
             g = 2 * lax.rem(n, 2)
 
+            @pl.when(n == 1)
+            def _():
+                tree_next(2, 1)
+                tree_next(1, 2)
+                kry_start(j - 1)
+
+            @pl.when(n == 3)
+            def _():
+                tree_next(2, 2)
+
             for c in range(NCHUNK):
                 @pl.when(n == 2 * c)
                 def _():
-                    for d in range(8):
-                        forward(c, d).wait_recv()
-            for c in range(1, NCHUNK):
-                @pl.when(n == 2 * c - 1)
-                def _():
-                    relay(c)
+                    for r in range(3):
+                        for m in range(8):
+                            forward(c, r, m).wait_recv()
 
             right_part(i, g, ya)
             right_part(i, g + 1, yb)
@@ -417,10 +452,12 @@
 
         lax.fori_loop(0, 6, body, 0)
         for i in range(NCHUNK):
-            forward(i, 0).wait_send()
-            for d in PEERS:
-                gather(i, d).wait_send()
-                forward(i, d).wait_send()
+            for r in range(3):
+                for m in range(8):
+                    forward(i, r, m).wait_send()
+                for ph in range(3):
+                    for c in tree(i, ph, r):
+                        c.wait_send()
         kry_wait(j - 1)
         vector_part(j)
         return carry
@@ -465,7 +502,7 @@
             pltpu.VMEM((8, 128), F32),
             dma((4, 3)), dma((NCHUNK, KLOC)), dma, dma((8,)), dma((8,)), dma((8,)), dma((8,)),
             dma((NCHUNK, 4, 2)), dma((NCHUNK, 4, 2)),
-            dma((NCHUNK, 8)), dma((NCHUNK, 8)), dma((NCHUNK, 8)), dma((NCHUNK, 8)),
+            dma((NCHUNK, 3, 7)), dma((NCHUNK, 3, 7)), dma((NCHUNK, 3, 8)), dma((NCHUNK, 3, 8)),
             dma, dma, dma((2, 16)), dma((2, 16)), dma((16,)), dma((16,)), dma,
         ],
         compiler_params=pltpu.CompilerParams(collective_id=0, has_side_effects=True, vmem_limit_bytes=60 * 1024 * 1024),

time: 355 us -> 336 us (0.946)
  Pallas kernels: 348 us -> 330 us
    pallas_call x1, Pallas kernels: 341 us -> 322 us  [run_steps(): pl.pallas_call(kernel, out_shape=(jax.ShapeDtypeStruct((STEPS, 16, ROWS,...]
where the time goes in v4:
time: 336 us
  Pallas kernels  330 us (98%)
    pallas_call x1, Pallas kernels, run_steps(): pl.pallas_call(kernel, out_shape=(jax.ShapeDtypeStruct((STEPS, 16, ROWS,...  322 us
    pallas_call x1, Pallas kernels, place_rows(): pl.pallas_call(place_kernel, grid=(STEPS + 1,), out_shape=jax.ShapeDtypeS...  7.76 us

profile of v4, /device:TPU:0, one launch (start us, length us, event | category | flops | bytes accessed | tf_op | source)
XLA Modules:
  0.0 335.9 jit_solution(16084177958623140521)
XLA Ops:
  0.7 0.7 broadcast_compare_fusion
  1.3 0.0 copy-start
  1.3 2.5 broadcast_select_fusion.r_ref
  3.9 0.0 copy-done
  3.9 0.6 pad.4.w_ref
  4.5 322.3 %lanczos.1 = (f32[6,16,24,384]{3,2,1,0:T(8,128)}, f32[6,8,128]{2,1,0:T(8,128)}, f32[6,8,128]{2,1,0:T(8,128)}, f32[384,384]{1,0:T(8,128)}) custom-call(f32[6144,384]{1,0:T(8,128)} %bitcast.3, bf16[4,384,384]{2,1,0:T(8,128)(2,1)} %l_ref.1, bf16[4,384,384]{2,1,0:T(8,128)(2,1)} %broadcast_select_fusion.r_ref, bf16[64,128]{1,0:T(8,128)(2,1)} %pad.4.w_ref), custom_call_target="tpu_custom_call" | custom-call | tf_op jit(solution)/shard_map/lanczos/pallas_call | solution.py:476
  326.8 1.4 slice_reduce_fusion
  328.2 7.8 %place_rows.1 = f32[7,24,16,384]{3,2,1,0:T(8,128)} custom-call(f32[24,16,384]{2,1,0:T(8,128)} %bitcast.4, f32[6,16,24,384]{3,2,1,0:T(8,128)} %get-tuple-element.8.block_ref), custom_call_target="tpu_custom_call" | custom-call | tf_op jit(solution)/shard_map/place_rows/pallas_call | solution.py:529
  (1 shorter events, 0.0 us)
Async XLA Ops:
  1.3 2.5 copy-start

commit v5 on v4

--- a/solution.py
+++ b/solution.py
@@ -40,9 +40,9 @@
     return scaled - 7 * lax.div(scaled, 8)
 
 
-def kernel(psi_ref, l_ref, r_ref, w_ref,
+def kernel(psi_ref, l_ref, r_ref, w_ref, flag_ref,
            kry_ref, alpha_ref, beta_ref, first_ref,
-           psi, u, lbuf, rbuf, wbuf, mbuf, ya, yb, z, sig, sig_in, wv, vcur, vprev, red, norm_v, delta_now, beta_now,
+           psi, u, lbuf, rsel, rbuf, wbuf, mbuf, ya, yb, z, sig, sig_in, wv, vcur, vprev, red, norm_v, delta_now, beta_now,
            psi_sem, ll_sem, loc_sem, rs_sem, rr_sem, ws_sem, wr_sem, ls_sem, lr_sem, gs_sem, gr_sem, fs_sem, fr_sem,
            xs_sem, xr_sem, ds_sem, dr_sem, ks_sem, kr_sem, kl_sem):
     me = lax.axis_index(AXIS)
@@ -59,7 +59,7 @@
 
     l_own = [[pltpu.make_async_copy(l_ref.at[k, :, pl.ds(CHUNK * i, CHUNK)], lbuf.at[i, :, pl.ds(CHUNK * k, CHUNK)], ll_sem.at[i, k])
               for k in range(KLOC)] for i in range(NCHUNK)]
-    r_own = pltpu.make_async_copy(r_ref.at[:, pl.ds(pl.multiple_of(COLS * chip, 16), COLS)], rbuf.at[0], loc_sem)
+    r_own = pltpu.make_async_copy(r_ref, rsel, loc_sem)
     part_rows = BOND * PAIR // 4
     psi_own = [[pltpu.make_async_copy(psi_ref.at[pl.ds(part_rows * i, part_rows), pl.ds(128 * c, 128)],
                                       psi.at[c, pl.ds(part_rows * i, part_rows)], psi_sem.at[i, c]) for c in range(3)]
@@ -77,7 +77,7 @@
     pl.semaphore_wait(barrier, 15)
 
     w_copies = {d: remote(w_ref, wbuf.at[d], ws_sem.at[d], wr_sem.at[d], peer(d)) for d in PEERS}
-    r_copies = {d: remote(r_ref.at[:, pl.ds(pl.multiple_of(COLS * flip(chip, d, 3), 16), COLS)], rbuf.at[d],
+    r_copies = {d: remote(rsel.at[:, pl.ds(pl.multiple_of(COLS * flip(chip, d, 3), 16), COLS)], rbuf.at[d],
                           rs_sem.at[d], rr_sem.at[d], peer(d)) for d in PEERS}
 
     def l_copies(i, n):
@@ -97,14 +97,20 @@
 
     for d in PEERS:
         w_copies[d].start()
-    for d in (1, 2, 4):
-        r_copies[d].start()
     for i in range(NCHUNK):
         for k in range(KLOC):
             l_own[i][k].wait()
         l_start(i, 0)
-    for d in (3, 5, 6, 7):
+
+    r_own.wait()
+    row_id = lax.broadcasted_iota(jnp.int32, (BOND, BOND), 0)
+    col_id = lax.broadcasted_iota(jnp.int32, (BOND, BOND), 1)
+    unit = jnp.where(row_id == col_id, 1.0, 0.0).astype(BF16)
+    for k in range(KLOC):
+        rsel[k] = jnp.where(jnp.full((BOND, BOND), flag_ref[k], jnp.int32) == 1, rsel[k].astype(F32), unit.astype(F32)).astype(BF16)
+    for d in PEERS:
         r_copies[d].start()
+    rbuf[0] = rsel[:, pl.ds(pl.multiple_of(COLS * chip, 16), COLS), :]
 
     wbuf[0] = w_ref[...]
     for d in PEERS:
@@ -112,8 +118,8 @@
     row_id = lax.broadcasted_iota(jnp.int32, (256, 16), 0)
     col_id = lax.broadcasted_iota(jnp.int32, (256, 16), 1)
     spread = jnp.where(lax.div(row_id, 16) == col_id, 1.0, 0.0).astype(BF16)
-    row_id = lax.broadcasted_iota(jnp.int32, (128, 256), 0)
-    col_id = lax.broadcasted_iota(jnp.int32, (128, 256), 1)
+    row_id = lax.broadcasted_iota(jnp.int32, (16, 256), 0)
+    col_id = lax.broadcasted_iota(jnp.int32, (16, 256), 1)
     spread_t = jnp.where(row_id == lax.div(col_id, 16), 1.0, 0.0).astype(BF16)
     row_id = lax.broadcasted_iota(jnp.int32, (256, 256), 0)
     col_id = lax.broadcasted_iota(jnp.int32, (256, 256), 1)
@@ -166,13 +172,17 @@
 
     def vector_part(j):
         lanes = pl.ds(pl.multiple_of(QROWS * core, 128), QROWS)
-        swap = remote(sig.at[:, pl.ds(pl.multiple_of(QROWS * (1 - core), 128), QROWS)], sig_in, xs_sem, xr_sem, partner)
-        swap.start()
+        other = pl.ds(pl.multiple_of(QROWS * (1 - core), 128), QROWS)
+        swaps = [remote(sig.at[pl.ds(96 * n, 96), other], sig_in.at[pl.ds(96 * n, 96)], xs_sem.at[n], xr_sem.at[n], partner)
+                 for n in range(4)]
+        for c in swaps:
+            c.start()
         beta_old = beta_now[0:1, 0:1]
-        swap.wait_recv()
         s_wv = jnp.zeros((8, 128), F32)
         s_cv = jnp.zeros((8, 128), F32)
         for n in range(BOND // COLS):
+            if n % 2 == 0:
+                swaps[n // 2].wait_recv()
             rows = pl.ds(COLS * n, COLS)
             w = sig[rows, lanes] + sig_in[rows, :]
             v = vcur[rows, :]
@@ -216,7 +226,8 @@
         norm_v[...] = jnp.zeros_like(norm_v)
         for c in copies:
             c.wait_send()
-        swap.wait_send()
+        for c in swaps:
+            c.wait_send()
 
     def advance(i):
         beta = beta_now[0:1, 0:1]
@@ -303,7 +314,6 @@
     vprev[...] = jnp.zeros_like(vprev)
     beta_now[...] = jnp.zeros_like(beta_now)
     sig[...] = jnp.zeros_like(sig)
-    r_own.wait()
     for i in range(NCHUNK):
         l_wait(i, 0)
         l_start(i, 1)
@@ -469,7 +479,7 @@
     kry_wait(STEPS - 1)
 
 
-def run_steps(psi, left_loc, r_in, w_in):
+def run_steps(psi, left_loc, right_loc, w_in, flag_loc):
     dma = pltpu.SemaphoreType.DMA
     vmem = pl.BlockSpec(memory_space=pltpu.VMEM)
     hbm = pl.BlockSpec(memory_space=pl.ANY)
@@ -479,14 +489,15 @@
                    jax.ShapeDtypeStruct((STEPS, 8, 128), F32),
                    jax.ShapeDtypeStruct((STEPS, 8, 128), F32),
                    jax.ShapeDtypeStruct((ROWS * PAIR, BOND), F32)),
-        in_specs=[hbm, hbm, hbm, vmem],
+        in_specs=[hbm, hbm, hbm, vmem, pl.BlockSpec(memory_space=pltpu.SMEM)],
         out_specs=(hbm, vmem, vmem, vmem),
         scratch_shapes=[
             pltpu.VMEM((3, BOND * PAIR, 128), F32),
             pltpu.VMEM((NCHUNK, BOND, PAIR * CHUNK), BF16),
             pltpu.VMEM((NCHUNK, BOND, CHIPS * KLOC * CHUNK), BF16),
+            pltpu.VMEM((KLOC, BOND, BOND), BF16),
             pltpu.VMEM((CHIPS, KLOC, COLS, BOND), BF16),
-            pltpu.VMEM((CHIPS, KLOC * 16, 128), BF16),
+            pltpu.VMEM((CHIPS, KLOC * 16, PAIR), BF16),
             pltpu.VMEM((CHIPS * KLOC, 256, 256), BF16),
             pltpu.VMEM((2 * KLOC * COLS, PAIR * CHUNK), BF16),
             pltpu.VMEM((2 * KLOC * COLS, PAIR * CHUNK), BF16),
@@ -503,47 +514,57 @@
             dma((4, 3)), dma((NCHUNK, KLOC)), dma, dma((8,)), dma((8,)), dma((8,)), dma((8,)),
             dma((NCHUNK, 4, 2)), dma((NCHUNK, 4, 2)),
             dma((NCHUNK, 3, 7)), dma((NCHUNK, 3, 7)), dma((NCHUNK, 3, 8)), dma((NCHUNK, 3, 8)),
-            dma, dma, dma((2, 16)), dma((2, 16)), dma((16,)), dma((16,)), dma,
+            dma((4,)), dma((4,)), dma((2, 16)), dma((2, 16)), dma((16,)), dma((16,)), dma,
         ],
         compiler_params=pltpu.CompilerParams(collective_id=0, has_side_effects=True, vmem_limit_bytes=60 * 1024 * 1024),
         name='lanczos',
-    )(psi, left_loc, r_in, w_in)
-
-
-def place_kernel(first_ref, block_ref, out_ref):
+    )(psi, left_loc, right_loc, w_in, flag_loc)
+
+
+def place_kernel(alpha_in, beta_in, first_ref, block_ref, out_ref, alpha_ref, beta_ref, tiles):
     j = pl.program_id(0)
 
     @pl.when(j == 0)
     def _():
         out_ref[0] = first_ref[...]
+        for n in range(STEPS):
+            alpha_ref[n] = alpha_in[n, 0, 0]
+            beta_ref[n] = beta_in[n, 0, 0]
 
     @pl.when(j > 0)
     def _():
         for h in range(2):
             for q in range(HALF):
-                pieces = [block_ref[0, 2 * c + h, :, COLS * q:COLS * q + COLS] for c in range(CHIPS)]
-                out_ref[0, :, HALF * h + q, :] = jnp.concatenate(pieces, axis=1)
-
-
-def place_rows(first, blocks):
+                row = jnp.concatenate([block_ref[0, 2 * c + h, :, COLS * q:COLS * q + COLS] for c in range(CHIPS)], axis=1)
+                for n in range(ROWS // 8):
+                    for t in range(3):
+                        tiles[t, pl.ds(8 * PAIR * n + HALF * h + q, 8, stride=PAIR), :] = row[8 * n:8 * n + 8, 128 * t:128 * t + 128]
+        for t in range(3):
+            out_ref[0, :, 128 * t:128 * t + 128] = tiles[t]
+
+
+def place_rows(alpha, beta, first, blocks):
+    smem = pl.BlockSpec(memory_space=pltpu.SMEM)
+    whole = pl.BlockSpec((STEPS, 8, 128), lambda j: (0, 0, 0))
     return pl.pallas_call(
         place_kernel,
         grid=(STEPS + 1,),
-        out_shape=jax.ShapeDtypeStruct((STEPS + 1, ROWS, PAIR, BOND), F32),
-        in_specs=[pl.BlockSpec((ROWS, PAIR, BOND), lambda j: (0, 0, 0)),
+        out_shape=(jax.ShapeDtypeStruct((STEPS + 1, ROWS * PAIR, BOND), F32),
+                   jax.ShapeDtypeStruct((STEPS,), F32), jax.ShapeDtypeStruct((STEPS,), F32)),
+        in_specs=[whole, whole, pl.BlockSpec((ROWS * PAIR, BOND), lambda j: (0, 0)),
                   pl.BlockSpec((1, 16, ROWS, BOND), lambda j: (jnp.maximum(j - 1, 0), 0, 0, 0))],
-        out_specs=pl.BlockSpec((1, ROWS, PAIR, BOND), lambda j: (j, 0, 0, 0)),
+        out_specs=(pl.BlockSpec((1, ROWS * PAIR, BOND), lambda j: (j, 0, 0)), smem, smem),
+        scratch_shapes=[pltpu.VMEM((3, ROWS * PAIR, 128), F32)],
         name='place_rows',
-    )(first, blocks)
+    )(alpha, beta, first, blocks)
 
 
 def solution(mesh):
     def device_body(psi, left_loc, pair_loc, right_loc, flag_loc):
-        r_in = jnp.where((flag_loc == 1)[:, None, None], right_loc, jnp.eye(BOND, dtype=BF16))
-        w_in = jnp.pad(pair_loc.reshape(KLOC * PAIR, PAIR), ((0, 0), (0, 128 - PAIR)))
-        blocks, alpha, beta, first = run_steps(psi.reshape(BOND * PAIR, BOND), left_loc, r_in, w_in)
-        krylov = place_rows(first.reshape(ROWS, PAIR, BOND), blocks)
-        return krylov, alpha[:, 0, 0], beta[:, 0, 0]
+        blocks, alpha, beta, first = run_steps(psi.reshape(BOND * PAIR, BOND), left_loc, right_loc,
+                                               pair_loc.reshape(KLOC * PAIR, PAIR), flag_loc)
+        krylov, alpha, beta = place_rows(alpha, beta, first, blocks)
+        return krylov.reshape(STEPS + 1, ROWS, PAIR, BOND), alpha, beta
 
     return jax.shard_map(device_body, mesh=mesh, in_specs=(P(), P(AXIS), P(AXIS), P(AXIS), P(AXIS)),
                          out_specs=(P(None, AXIS), P(), P()), check_vma=False)

time: 336 us -> 331 us (0.985)
  no operation moved by 1% of the time
where the time goes in v5:
time: 331 us; the launch traced here: 330 us
  Pallas kernels  329 us (99%)
    pallas_call x1, Pallas kernels, run_steps(): pl.pallas_call(kernel, out_shape=(jax.ShapeDtypeStruct((STEPS, 16, ROWS,...  322 us
    pallas_call x1, Pallas kernels, place_rows(): pl.pallas_call(place_kernel, grid=(STEPS + 1,), out_shape=(jax.ShapeDtype...  7.91 us

profile of v5, /device:TPU:0, one launch (start us, length us, event | category | flops | bytes accessed | tf_op | source)
XLA Modules:
  0.0 330.2 jit_solution(7137263085315671186)
XLA Ops:
  0.6 321.6 %lanczos.1 = (f32[6,16,24,384]{3,2,1,0:T(8,128)}, f32[6,8,128]{2,1,0:T(8,128)}, f32[6,8,128]{2,1,0:T(8,128)}, f32[384,384]{1,0:T(8,128)}) custom-call(f32[6144,384]{1,0:T(8,128)} %bitcast.3, bf16[4,384,384]{2,1,0:T(8,128)(2,1)} %l_ref.1, bf16[4,384,384]{2,1,0:T(8,128)(2,1)} %r_ref.1, bf16[64,16]{1,0:T(8,128)(2,1)} %bitcast.4, s32[4]{0:T(128)} %flag_ref.1), custom_call_target="tpu_custom_call" | custom-call | tf_op jit(solution)/shard_map/lanczos/pallas_call | solution.py:486
  322.2 7.9 %place_rows.1 = (f32[7,384,384]{2,1,0:T(8,128)}, f32[6]{0:T(128)}, f32[6]{0:T(128)}) custom-call(f32[6,8,128]{2,1,0:T(8,128)} %get-tuple-element.10.alpha_in, f32[6,8,128]{2,1,0:T(8,128)} %get-tuple-element.11.beta_in, f32[384,384]{1,0:T(8,128)} %get-tuple-element.12.first_ref, f32[6,16,24,384]{3,2,1,0:T(8,128)} %get-tuple-element.13.block_ref), custom_call_target="tpu_custom_call" | custom-call | tf_op jit(solution)/shard_map/place_rows/pallas_call | solution.py:549

commit v6 on v5

--- a/solution.py
+++ b/solution.py
@@ -36,14 +36,16 @@
 
 
 def rotl(pos, chunk):
+    if isinstance(pos, int) and isinstance(chunk, int):
+        return (pos << chunk) - 7 * ((pos << chunk) // 8)
     scaled = pos * (1 + chunk + lax.div(chunk, 2)) if not isinstance(chunk, int) else pos * (1 << chunk)
     return scaled - 7 * lax.div(scaled, 8)
 
 
 def kernel(psi_ref, l_ref, r_ref, w_ref, flag_ref,
            kry_ref, alpha_ref, beta_ref, first_ref,
-           psi, u, lbuf, rsel, rbuf, wbuf, mbuf, ya, yb, z, sig, sig_in, wv, vcur, vprev, red, norm_v, delta_now, beta_now,
-           psi_sem, ll_sem, loc_sem, rs_sem, rr_sem, ws_sem, wr_sem, ls_sem, lr_sem, gs_sem, gr_sem, fs_sem, fr_sem,
+           psi, u, lbuf, rsel, rbuf, wbuf, mbuf, ya, yb, yc, yd, z, sig, sig_in, wv, vcur, vprev, red, norm_v, delta_now, beta_now,
+           psi_sem, ll_sem, loc_sem, rs_sem, rr_sem, ws_sem, wr_sem, ls_sem, lr_sem, ns_sem, nr_sem, gs_sem, gr_sem, fs_sem, fr_sem,
            xs_sem, xr_sem, ds_sem, dr_sem, ks_sem, kr_sem, kl_sem):
     me = lax.axis_index(AXIS)
     chip = lax.div(me, 2)
@@ -134,30 +136,29 @@
 
     lax.fori_loop(0, CHIPS, build, 0)
 
-    def right_part(i, g, y):
+    def right_part(i, g, y, tiles=range(8)):
         slot_a = rotl(2 * g, i)
         slot_b = rotl(2 * g + 1, i)
         right = jnp.concatenate([rbuf[slot_a].reshape(KLOC * COLS, BOND), rbuf[slot_b].reshape(KLOC * COLS, BOND)], axis=0)
-        for n in range(8):
+        for n in tiles:
             lanes = pl.ds(256 * n, 256)
-            y[:, lanes] = jnp.dot(right, u[i, :, lanes], preferred_element_type=F32).astype(BF16)
+            both = jnp.dot(right, u[i, :, lanes], preferred_element_type=F32).astype(BF16)
+            y[2 * n] = both[:, 0:128]
+            y[2 * n + 1] = both[:, 128:256]
 
     def pair_part(i, g, y, slot):
         slot_a = rotl(2 * g, i)
         slot_b = rotl(2 * g + 1, i)
         for kk in range(8):
             mat = mbuf[(slot_a if kk < KLOC else slot_b) * KLOC + kk % KLOC]
-            cols = [jnp.concatenate([y[COLS * kk + 16 * t:COLS * kk + 16 * t + 16, 128 * r:128 * r + 128]
-                                     for r in range(PAIR)], axis=0) for t in range(3)]
+            cols = [y[:, pl.ds(COLS * kk + 16 * t, 16), :].reshape(PAIR * 16, CHUNK) for t in range(3)]
             pair = jnp.dot(mat, jnp.concatenate(cols, axis=1), preferred_element_type=F32).astype(BF16)
-            for q in range(PAIR):
-                for t in range(3):
-                    z[slot, COLS * q + 16 * t:COLS * q + 16 * t + 16, 128 * kk:128 * kk + 128] = \
-                        pair[16 * q:16 * q + 16, 128 * t:128 * t + 128]
+            for t in range(3):
+                z[slot, :, pl.ds(16 * t, 16), pl.ds(128 * kk, 128)] = pair[:, 128 * t:128 * t + 128].reshape(PAIR, 16, CHUNK)
 
     def left_part(i, g, slot):
         left = lbuf[i, :, pl.ds(pl.multiple_of(g * 1024, 1024), 1024)]
-        sig[...] += lax.dot_general(left, z[slot], (((1,), (1,)), ((), ())), preferred_element_type=F32)
+        sig[...] += lax.dot_general(left, z[slot].reshape(PAIR * COLS, 2 * KLOC * CHUNK), (((1,), (1,)), ((), ())), preferred_element_type=F32)
 
     def fold(x):
         out = x[0:8, 0:128]
@@ -375,99 +376,139 @@
                 c.wait_send()
     vector_part(0)
 
-    def region(i, c, r):
-        return u.at[i, pl.ds(pl.multiple_of(COLS * c + 16 * r, 16), 16), pl.ds(pl.multiple_of(HALF * CHUNK * core, 1024), HALF * CHUNK)]
-
-    def axis_of(r, ph):
-        return 1 << ((r + ph) % 3)
-
-    def masks(r, ph):
-        out = [0]
-        for n in range(ph):
-            out += [m ^ axis_of(r, n) for m in out]
-        return out
-
-    def tree(i, ph, r):
-        out = []
-        for n, m in enumerate(masks(r, ph)):
-            src = region(i, flip(chip, m, 3), r)
-            num = (1 << ph) - 1 + n
-            out.append(remote(src, src, gs_sem.at[i, r, num], gr_sem.at[i, r, num], peer(axis_of(r, ph))))
-        return out
-
-    def forward(i, r, m):
-        src = region(i, flip(chip, m, 3), r)
-        return remote(src, src, fs_sem.at[i, r, m], fr_sem.at[i, r, m], partner)
-
-    def tree_start(i, ph):
-        for r in range(3):
-            for c in tree(i, ph, r):
-                c.start()
-
-    def tree_next(i, ph):
-        for r in range(3):
-            for c in tree(i, ph, r):
-                c.wait_recv()
-            if ph < 2:
-                for c in tree(i, ph + 1, r):
-                    c.start()
-            for m in masks(r, ph):
-                forward(i, r, m ^ axis_of(r, ph)).start()
+    units = ((0, 0, 512), (0, 512, 512), (1, 0, 1024), (2, 0, 1024))
+
+    def region(un, mask, lo, width):
+        i, first, _ = units[un]
+        return u.at[i, pl.ds(pl.multiple_of(COLS * flip(chip, mask, 3), 16), COLS),
+                    pl.ds(pl.multiple_of(HALF * CHUNK * core + first + lo, 128), width)]
+
+    def near(un, a):
+        own = region(un, 0, 0, units[un][2])
+        return remote(own, own, ns_sem.at[un, a], nr_sem.at[un, a], peer(1 << a))
+
+    def far(un):
+        own = region(un, 0, 0, units[un][2])
+        return remote(own, own, ns_sem.at[un, 3], nr_sem.at[un, 3], peer(7))
+
+    def second(un, a, h):
+        half = units[un][2] // 2
+        block = region(un, 1 << a, half * h, half)
+        return remote(block, block, gs_sem.at[un, 2 * a + h], gr_sem.at[un, 2 * a + h], peer(1 << ((a + 1 + h) % 3)))
+
+    def cross(un, n):
+        width = units[un][2]
+        if n < 5:
+            block = region(un, (0, 1, 2, 4, 7)[n], 0, width)
+        else:
+            a, h = divmod(n - 5, 2)
+            block = region(un, (1 << a) ^ (1 << ((a + 1 + h) % 3)), width // 2 * h, width // 2)
+        return remote(block, block, fs_sem.at[un, n], fr_sem.at[un, n], partner)
+
+    def send_out(un):
+        for a in range(3):
+            near(un, a).start()
+        far(un).start()
+        cross(un, 0).start()
+
+    def hop(un):
+        for a in range(3):
+            near(un, a).wait_recv()
+            second(un, a, 0).start()
+            second(un, a, 1).start()
+            cross(un, 1 + a).start()
+
+    def land(un):
+        far(un).wait_recv()
+        cross(un, 4).start()
+        for a in range(3):
+            for h in range(2):
+                second(un, a, h).wait_recv()
+                cross(un, 5 + 2 * a + h).start()
+
+    def ready(un):
+        for n in range(11):
+            cross(un, n).wait_recv()
+
+    def sent(un):
+        for a in range(3):
+            near(un, a).wait_send()
+        far(un).wait_send()
+        for a in range(3):
+            for h in range(2):
+                second(un, a, h).wait_send()
+        for n in range(11):
+            cross(un, n).wait_send()
+
+    def publish(i):
+        flat = advance(i).astype(BF16).T
+        for q in range(HALF):
+            u[i, pl.ds(pl.multiple_of(COLS * chip, 16), COLS),
+              pl.ds(pl.multiple_of(HALF * CHUNK * core + CHUNK * q, 128), CHUNK)] = flat[COLS * q:COLS * q + COLS, :]
 
     def step_body(j, carry):
-        for i in range(NCHUNK):
-            flat = advance(i).astype(BF16).T
-            for q in range(HALF):
-                u[i, pl.ds(pl.multiple_of(COLS * chip, 16), COLS),
-                  pl.ds(pl.multiple_of(HALF * CHUNK * core + CHUNK * q, 128), CHUNK)] = flat[COLS * q:COLS * q + COLS, :]
-            tree_start(i, 0)
-            for r in range(3):
-                forward(i, r, 0).start()
+        publish(0)
+        send_out(0)
+        send_out(1)
+        publish(1)
+        publish(2)
         sig[...] = jnp.zeros_like(sig)
-        tree_next(0, 0)
-        tree_next(1, 0)
-        tree_next(0, 1)
-        tree_next(1, 1)
-        tree_next(2, 0)
-        tree_next(0, 2)
+        hop(0)
+        hop(1)
+        send_out(2)
+        land(0)
+        ready(0)
+        for g, y in enumerate((ya, yb, yc, yd)):
+            right_part(0, g, y, (0, 1, 4, 5))
+        land(1)
+        ready(1)
+        right_part(0, 0, ya, (2, 3, 6, 7))
+        right_part(0, 1, yb, (2, 3, 6, 7))
+        hop(2)
+        send_out(3)
+        pair_part(0, 0, ya, 0)
+        left_part(0, 0, 0)
+        pair_part(0, 1, yb, 1)
+        left_part(0, 1, 1)
+        right_part(0, 2, yc, (2, 3, 6, 7))
+        right_part(0, 3, yd, (2, 3, 6, 7))
+        pair_part(0, 2, yc, 0)
+        left_part(0, 2, 0)
+        land(2)
+        pair_part(0, 3, yd, 1)
+        left_part(0, 3, 1)
+        ready(2)
 
         def body(n, carry):
             i = lax.div(n, 2)
             g = 2 * lax.rem(n, 2)
 
-            @pl.when(n == 1)
+            @pl.when(n == 4)
             def _():
-                tree_next(2, 1)
-                tree_next(1, 2)
-                kry_start(j - 1)
+                ready(3)
+
+            right_part(i, g, ya)
+            right_part(i, g + 1, yb)
+
+            pair_part(i, g, ya, 0)
+            left_part(i, g, 0)
+
+            @pl.when(n == 2)
+            def _():
+                hop(3)
 
             @pl.when(n == 3)
             def _():
-                tree_next(2, 2)
-
-            for c in range(NCHUNK):
-                @pl.when(n == 2 * c)
-                def _():
-                    for r in range(3):
-                        for m in range(8):
-                            forward(c, r, m).wait_recv()
-
-            right_part(i, g, ya)
-            right_part(i, g + 1, yb)
-            pair_part(i, g, ya, 0)
-            left_part(i, g, 0)
+                land(3)
+                kry_start(j - 1)
+
             pair_part(i, g + 1, yb, 1)
             left_part(i, g + 1, 1)
             return carry
 
-        lax.fori_loop(0, 6, body, 0)
-        for i in range(NCHUNK):
-            for r in range(3):
-                for m in range(8):
-                    forward(i, r, m).wait_send()
-                for ph in range(3):
-                    for c in tree(i, ph, r):
-                        c.wait_send()
+        lax.fori_loop(2, 6, body, 0)
+        for un in range(4):
+            sent(un)
         kry_wait(j - 1)
         vector_part(j)
         return carry
@@ -499,9 +540,11 @@
             pltpu.VMEM((CHIPS, KLOC, COLS, BOND), BF16),
             pltpu.VMEM((CHIPS, KLOC * 16, PAIR), BF16),
             pltpu.VMEM((CHIPS * KLOC, 256, 256), BF16),
-            pltpu.VMEM((2 * KLOC * COLS, PAIR * CHUNK), BF16),
-            pltpu.VMEM((2 * KLOC * COLS, PAIR * CHUNK), BF16),
-            pltpu.VMEM((12, PAIR * COLS, 2 * KLOC * CHUNK), BF16),
+            pltpu.VMEM((PAIR, 2 * KLOC * COLS, CHUNK), BF16),
+            pltpu.VMEM((PAIR, 2 * KLOC * COLS, CHUNK), BF16),
+            pltpu.VMEM((PAIR, 2 * KLOC * COLS, CHUNK), BF16),
+            pltpu.VMEM((PAIR, 2 * KLOC * COLS, CHUNK), BF16),
+            pltpu.VMEM((12, PAIR, COLS, 2 * KLOC * CHUNK), BF16),
             pltpu.VMEM((BOND, PAIR * COLS), F32),
             pltpu.VMEM((BOND, QROWS), F32),
             pltpu.VMEM((BOND, QROWS), F32),
@@ -513,7 +556,7 @@
             pltpu.VMEM((8, 128), F32),
             dma((4, 3)), dma((NCHUNK, KLOC)), dma, dma((8,)), dma((8,)), dma((8,)), dma((8,)),
             dma((NCHUNK, 4, 2)), dma((NCHUNK, 4, 2)),
-            dma((NCHUNK, 3, 7)), dma((NCHUNK, 3, 7)), dma((NCHUNK, 3, 8)), dma((NCHUNK, 3, 8)),
+            dma((4, 4)), dma((4, 4)), dma((4, 6)), dma((4, 6)), dma((4, 11)), dma((4, 11)),
             dma((4,)), dma((4,)), dma((2, 16)), dma((2, 16)), dma((16,)), dma((16,)), dma,
         ],
         compiler_params=pltpu.CompilerParams(collective_id=0, has_side_effects=True, vmem_limit_bytes=60 * 1024 * 1024),

time: 331 us -> 322 us (0.973)
  Pallas kernels: 329 us -> 321 us
    pallas_call x1, Pallas kernels: 322 us -> 313 us  [run_steps(): pl.pallas_call(kernel, out_shape=(jax.ShapeDtypeStruct((STEPS, 16, ROWS,...]
where the time goes in v6:
time: 322 us; the launch traced here: 321 us
  Pallas kernels  321 us (100%)
    pallas_call x1, Pallas kernels, run_steps(): pl.pallas_call(kernel, out_shape=(jax.ShapeDtypeStruct((STEPS, 16, ROWS,...  313 us
    pallas_call x1, Pallas kernels, place_rows(): pl.pallas_call(place_kernel, grid=(STEPS + 1,), out_shape=(jax.ShapeDtype...  7.91 us

profile of v6, /device:TPU:0, one launch (start us, length us, event | category | flops | bytes accessed | tf_op | source)
XLA Modules:
  0.0 321.4 jit_solution(854752806189032817)
XLA Ops:
  0.6 312.7 %lanczos.1 = (f32[6,16,24,384]{3,2,1,0:T(8,128)}, f32[6,8,128]{2,1,0:T(8,128)}, f32[6,8,128]{2,1,0:T(8,128)}, f32[384,384]{1,0:T(8,128)}) custom-call(f32[6144,384]{1,0:T(8,128)} %bitcast.3, bf16[4,384,384]{2,1,0:T(8,128)(2,1)} %l_ref.1, bf16[4,384,384]{2,1,0:T(8,128)(2,1)} %r_ref.1, bf16[64,16]{1,0:T(8,128)(2,1)} %bitcast.4, s32[4]{0:T(128)} %flag_ref.1), custom_call_target="tpu_custom_call" | custom-call | tf_op jit(solution)/shard_map/lanczos/pallas_call | solution.py:527
  313.4 7.9 %place_rows.1 = (f32[7,384,384]{2,1,0:T(8,128)}, f32[6]{0:T(128)}, f32[6]{0:T(128)}) custom-call(f32[6,8,128]{2,1,0:T(8,128)} %get-tuple-element.10.alpha_in, f32[6,8,128]{2,1,0:T(8,128)} %get-tuple-element.11.beta_in, f32[384,384]{1,0:T(8,128)} %get-tuple-element.12.first_ref, f32[6,16,24,384]{3,2,1,0:T(8,128)} %get-tuple-element.13.block_ref), custom_call_target="tpu_custom_call" | custom-call | tf_op jit(solution)/shard_map/place_rows/pallas_call | solution.py:592

commit v7 on v6

--- a/solution.py
+++ b/solution.py
@@ -22,7 +22,7 @@
 F32 = jnp.float32
 BF16 = jnp.bfloat16
 PEERS = (1, 2, 4, 3, 5, 6, 7)
-FORWARD_AT = 3
+FORWARD_AT = 2
 
 
 def flip(idx, mask, bits):
@@ -293,6 +293,9 @@
 
         return carry
 
+    for i in range(NCHUNK):
+        l_wait(i, 0)
+        l_start(i, 1)
     lax.fori_loop(0, PAIR, spread_pair, 0)
     start = jnp.zeros((8, 128), F32)
     for i in range(NCHUNK):
@@ -315,9 +318,6 @@
     vprev[...] = jnp.zeros_like(vprev)
     beta_now[...] = jnp.zeros_like(beta_now)
     sig[...] = jnp.zeros_like(sig)
-    for i in range(NCHUNK):
-        l_wait(i, 0)
-        l_start(i, 1)
     for d in PEERS:
         r_copies[d].wait_recv()
 
@@ -564,40 +564,55 @@
     )(psi, left_loc, right_loc, w_in, flag_loc)
 
 
-def place_kernel(alpha_in, beta_in, first_ref, block_ref, out_ref, alpha_ref, beta_ref, tiles):
-    j = pl.program_id(0)
-
-    @pl.when(j == 0)
-    def _():
-        out_ref[0] = first_ref[...]
-        for n in range(STEPS):
-            alpha_ref[n] = alpha_in[n, 0, 0]
-            beta_ref[n] = beta_in[n, 0, 0]
-
-    @pl.when(j > 0)
-    def _():
+def place_kernel(alpha_in, beta_in, first_ref, block_ref, out_ref, alpha_ref, beta_ref, blocks, rows, tiles, in_sem, out_sem):
+    def get(j):
+        return pltpu.make_async_copy(block_ref.at[j], blocks.at[j], in_sem.at[j])
+
+    def put(j):
+        return pltpu.make_async_copy(rows.at[j], out_ref.at[j], out_sem.at[j])
+
+    first = pltpu.make_async_copy(first_ref, rows.at[0], in_sem.at[STEPS])
+    for j in range(STEPS):
+        get(j).start()
+    first.start()
+    for n in range(STEPS):
+        alpha_ref[n] = alpha_in[n, 0, 0]
+        beta_ref[n] = beta_in[n, 0, 0]
+
+    def body(j, carry):
+        get(j).wait()
         for h in range(2):
             for q in range(HALF):
-                row = jnp.concatenate([block_ref[0, 2 * c + h, :, COLS * q:COLS * q + COLS] for c in range(CHIPS)], axis=1)
+                row = jnp.concatenate([blocks[j, 2 * c + h, :, COLS * q:COLS * q + COLS] for c in range(CHIPS)], axis=1)
                 for n in range(ROWS // 8):
                     for t in range(3):
                         tiles[t, pl.ds(8 * PAIR * n + HALF * h + q, 8, stride=PAIR), :] = row[8 * n:8 * n + 8, 128 * t:128 * t + 128]
         for t in range(3):
-            out_ref[0, :, 128 * t:128 * t + 128] = tiles[t]
+            rows[j + 1, :, 128 * t:128 * t + 128] = tiles[t]
+        put(j + 1).start()
+        return carry
+
+    lax.fori_loop(0, STEPS, body, 0)
+    first.wait()
+    put(0).start()
+    for j in range(STEPS + 1):
+        put(j).wait()
 
 
 def place_rows(alpha, beta, first, blocks):
     smem = pl.BlockSpec(memory_space=pltpu.SMEM)
-    whole = pl.BlockSpec((STEPS, 8, 128), lambda j: (0, 0, 0))
+    vmem = pl.BlockSpec(memory_space=pltpu.VMEM)
+    hbm = pl.BlockSpec(memory_space=pl.ANY)
     return pl.pallas_call(
         place_kernel,
-        grid=(STEPS + 1,),
         out_shape=(jax.ShapeDtypeStruct((STEPS + 1, ROWS * PAIR, BOND), F32),
                    jax.ShapeDtypeStruct((STEPS,), F32), jax.ShapeDtypeStruct((STEPS,), F32)),
-        in_specs=[whole, whole, pl.BlockSpec((ROWS * PAIR, BOND), lambda j: (0, 0)),
-                  pl.BlockSpec((1, 16, ROWS, BOND), lambda j: (jnp.maximum(j - 1, 0), 0, 0, 0))],
-        out_specs=(pl.BlockSpec((1, ROWS * PAIR, BOND), lambda j: (j, 0, 0)), smem, smem),
-        scratch_shapes=[pltpu.VMEM((3, ROWS * PAIR, 128), F32)],
+        in_specs=[vmem, vmem, hbm, hbm],
+        out_specs=(hbm, smem, smem),
+        scratch_shapes=[pltpu.VMEM((STEPS, 16, ROWS, BOND), F32), pltpu.VMEM((STEPS + 1, ROWS * PAIR, BOND), F32),
+                        pltpu.VMEM((3, ROWS * PAIR, 128), F32),
+                        pltpu.SemaphoreType.DMA((STEPS + 1,)), pltpu.SemaphoreType.DMA((STEPS + 1,))],
+        compiler_params=pltpu.CompilerParams(vmem_limit_bytes=60 * 1024 * 1024),
         name='place_rows',
     )(alpha, beta, first, blocks)
 

time: 322 us -> 320 us (level)
  no operation moved by 1% of the time
where the time goes in v7:
time: 320 us
  Pallas kernels  319 us (100%)
    pallas_call x1, Pallas kernels, run_steps(): pl.pallas_call(kernel, out_shape=(jax.ShapeDtypeStruct((STEPS, 16, ROWS,...  312 us
    pallas_call x1, Pallas kernels, place_rows(): pl.pallas_call(place_kernel, out_shape=(jax.ShapeDtypeStruct((STEPS + 1,...  7.07 us

profile of v7, /device:TPU:0, one launch (start us, length us, event | category | flops | bytes accessed | tf_op | source)
XLA Modules:
  0.0 319.9 jit_solution(13138598764862250110)
XLA Ops:
  0.6 312.0 %lanczos.1 = (f32[6,16,24,384]{3,2,1,0:T(8,128)}, f32[6,8,128]{2,1,0:T(8,128)}, f32[6,8,128]{2,1,0:T(8,128)}, f32[384,384]{1,0:T(8,128)}) custom-call(f32[6144,384]{1,0:T(8,128)} %bitcast.3, bf16[4,384,384]{2,1,0:T(8,128)(2,1)} %l_ref.1, bf16[4,384,384]{2,1,0:T(8,128)(2,1)} %r_ref.1, bf16[64,16]{1,0:T(8,128)(2,1)} %bitcast.4, s32[4]{0:T(128)} %flag_ref.1), custom_call_target="tpu_custom_call" | custom-call | tf_op jit(solution)/shard_map/lanczos/pallas_call | solution.py:527
  312.7 7.1 %place_rows.1 = (f32[7,384,384]{2,1,0:T(8,128)}, f32[6]{0:T(128)}, f32[6]{0:T(128)}) custom-call(f32[6,8,128]{2,1,0:T(8,128)} %get-tuple-element.10.alpha_in, f32[6,8,128]{2,1,0:T(8,128)} %get-tuple-element.11.beta_in, f32[384,384]{1,0:T(8,128)} %get-tuple-element.12.first_ref, f32[6,16,24,384]{3,2,1,0:T(8,128)} %get-tuple-element.13.block_ref), custom_call_target="tpu_custom_call" | custom-call | tf_op jit(solution)/shard_map/place_rows/pallas_call | solution.py:606
